TPU v7x, 32 devices: a whole 2x2x4 slice. The times are simulated.
32 devices in a mesh: band: 4 (over z), ga: 8 (over y, x, core).
Axes of the slice: x: 2, y: 2, z: 4, core: 2. Of those that a mesh axis runs over, the one named last changes fastest.
Arguments:
- coeffs: float32 [2, 4, 18432], P(None, 'band', 'ga'), may hold values from -8 to 8
- cell_map: int32 [18432], P('ga'), may hold values from 0 to 110591, as said below
- potential: float32 [96, 96, 96], P(None, 'ga'), may hold values from -2 to 1
- projectors: float32 [2, 64, 18432], P(None, None, 'ga'), may hold values from -6 to 6
- strengths: float32 [8, 8, 8], replicated, may hold values from -2 to 2
- proj_atom: int32 [64], replicated, may hold values from 0 to 7, as said below
- proj_chan: int32 [64], replicated, may hold values from 0 to 7, as said below
Outputs:
- new_bands: float32 [2, 4, 18432], P(None, 'band', 'ga')
- energy: float32 [4], P('band')
- residual_norm: float32 [4], P('band')
- correlation: float32 [2, 4, 4], P(None, 'band')
- subspace: float32 [2, 4, 4], P(None, 'band')
Inputs may be any that keep to these rules, and one draw needn't show every extreme that they name: `cell_map`: in block d (entries d * 2304 to (d + 1) * 2304 - 1) the entries are distinct cells (i * 96 + y) * 96 + z of grid planes x = d + 8 * i. `proj_atom`: each pair of atom and channel belongs to exactly one projector. `proj_chan`: each pair of atom and channel belongs to exactly one projector.
All inputs are finite; a program needn't handle non-finite values.
Results may differ from a plain program's by a relative error of at most 0.0002.
Values sent between devices are 32-bit elements; how exact they have to be, the bound alone decides.
A program may use at most 64 MiB of HBM per device.

v0:
```python
import functools

import jax
import jax.numpy as jnp
import numpy as np
from jax import lax
from jax.experimental import pallas as pl
from jax.experimental.pallas import tpu as pltpu
from jax.sharding import PartitionSpec as P

top_precision = lax.Precision.HIGHEST
kin_unit = 0.02
small_eps = 1e-06


def signed_freq(index_arr, grid_len):
    return jnp.where(index_arr < grid_len // 2, index_arr, index_arr - grid_len)


def wave_tables(grid_len, row_freq, col_freq, sign_val, factor):
    phase = row_freq[:, None] * col_freq[None, :] % grid_len
    angle = 2.0 * jnp.pi / grid_len * phase.astype(jnp.float32)
    return (jnp.cos(angle) * factor, jnp.sin(angle) * (sign_val * factor))


def block_table(cos_table, sin_table):
    upper = jnp.concatenate([cos_table, sin_table], axis=1)
    lower = jnp.concatenate([-sin_table, cos_table], axis=1)
    return jnp.concatenate([upper, lower], axis=0)


def quarter_turn(grid_vals):
    half_len = grid_vals.shape[-1] // 2
    return jnp.concatenate([-grid_vals[..., half_len:], grid_vals[..., :half_len]], axis=-1)


def mix_dim(grid_vals, cos_table, sin_table, pattern):
    direct = jnp.einsum(pattern, cos_table, grid_vals, precision=top_precision)
    turned = jnp.einsum(pattern, sin_table, quarter_turn(grid_vals), precision=top_precision)
    return direct + turned


def mix_last(grid_vals, table_full):
    row_width = grid_vals.shape[-1]
    product = jnp.dot(
        grid_vals.reshape(-1, row_width),
        table_full,
        precision=top_precision,
        preferred_element_type=jnp.float32,
    )
    return product.reshape(grid_vals.shape)


def band_dot(left_vec, right_vec, weight):
    return jnp.sum(left_vec * right_vec * weight, axis=(0, 2))


def per_band(values):
    return values[None, :, None]


def pair_products(left_vec, right_vec):

    def contract(first_part, second_part):
        return jnp.einsum("bg,cg->bc", first_part, second_part, precision=top_precision)

    real_part = contract(left_vec[0], right_vec[0]) + contract(left_vec[1], right_vec[1])
    imag_part = contract(left_vec[0], right_vec[1]) - contract(left_vec[1], right_vec[0])
    return jnp.stack([real_part, imag_part])


def precondition(residual, kinetic, kin_level):
    x_ratio = kinetic[None, :] / (1.5 * kin_level[:, None] + 1.0)
    numer_poly = 27.0 + x_ratio * (18.0 + x_ratio * (12.0 + 8.0 * x_ratio))
    square = x_ratio * x_ratio
    return residual * (numer_poly / (numer_poly + 16.0 * square * square))[None]


def coupling_matrix(proj_atom, proj_chan, strengths):
    atom_count = strengths.shape[0]
    chan_count = strengths.shape[1]
    symmetric = 0.5 * (strengths + jnp.swapaxes(strengths, 1, 2))
    atom_hot = (proj_atom[:, None] == jnp.arange(atom_count, dtype=jnp.int32)[None, :]).astype(
        jnp.float32
    )
    chan_hot = (proj_chan[:, None] == jnp.arange(chan_count, dtype=jnp.int32)[None, :]).astype(
        jnp.float32
    )
    rows_d = jnp.einsum("pa,pc,acd->pd", atom_hot, chan_hot, symmetric, precision=top_precision)
    same_atom = jnp.dot(
        atom_hot, atom_hot.T, precision=top_precision, preferred_element_type=jnp.float32
    )
    return same_atom * jnp.dot(
        rows_d, chan_hot.T, precision=top_precision, preferred_element_type=jnp.float32
    )


def combine(term_list):
    merged = {}
    for scalar, coef_map in term_list:
        for index_one, coef_a in coef_map.items():
            merged[index_one] = merged.get(index_one, 0.0) + scalar * coef_a
    return merged


def gram_form(gram_table, left_map, right_map, use_kin):
    running = 0.0
    for index_one, coef_a in left_map.items():
        for index_two, coef_b in right_map.items():
            running = running + coef_a * coef_b * gram_table[use_kin, index_one, index_two]
    return running


def new_pairs(first_new, last_new, kinds):
    pair_list = []
    for use_kin in kinds:
        for index_two in range(first_new, last_new):
            for index_one in range(index_two + 1):
                pair_list.append((index_one, index_two, use_kin))
    return pair_list


def plain_body(coeffs, cell_map, potential, projectors, strengths, proj_atom, proj_chan):
    ga_count = lax.axis_size("ga")
    grid_len = potential.shape[0]
    planes = grid_len // ga_count
    band_local = coeffs.shape[1]
    total_pw = coeffs.shape[2] * ga_count
    device = lax.axis_index("ga")
    plane_num = cell_map // (grid_len * grid_len)
    y_index = cell_map // grid_len % grid_len
    z_index = cell_map % grid_len
    freq_x = signed_freq(device + ga_count * plane_num, grid_len)
    freq_y = signed_freq(y_index, grid_len)
    freq_z = signed_freq(z_index, grid_len)
    kinetic = kin_unit * (freq_x * freq_x + freq_y * freq_y + freq_z * freq_z).astype(jnp.float32)
    kin_weight = kinetic[None, None, :]
    slot_re = (plane_num * grid_len + y_index) * (2 * grid_len) + z_index
    slot_im = slot_re + grid_len
    cell_count = planes * grid_len * 2 * grid_len
    natural = jnp.arange(grid_len, dtype=jnp.int32)
    cyclic = natural % planes * ga_count + natural // planes
    cos_fwd, sin_fwd = wave_tables(grid_len, natural, natural, 1.0, 1.0)
    cos_back, sin_back = wave_tables(grid_len, natural, natural, -1.0, 1.0 / grid_len)
    z_forward = block_table(cos_fwd, sin_fwd)
    z_backward = block_table(cos_back, sin_back)
    xcos_fwd, xsin_fwd = wave_tables(grid_len, natural, cyclic, 1.0, 1.0)
    xcos_back, xsin_back = wave_tables(grid_len, cyclic, natural, -1.0, 1.0 / grid_len)
    doubled = jnp.concatenate([potential, potential], axis=-1)
    coupling = coupling_matrix(proj_atom, proj_chan, strengths)

    def real_space(grid_vals):
        grid_vals = mix_dim(grid_vals, xcos_fwd, xsin_fwd, "kj,bjyw->bkyw")
        grid_vals = grid_vals * doubled[None]
        grid_vals = mix_dim(grid_vals, xcos_back, xsin_back, "jk,bkyw->bjyw")
        return lax.all_to_all(grid_vals, "ga", split_axis=1, concat_axis=2, tiled=True)

    def local_part(vectors):
        item_count = vectors.shape[1]
        flat_grid = jnp.zeros((item_count, cell_count), jnp.float32)
        flat_grid = flat_grid.at[:, slot_re].set(vectors[0]).at[:, slot_im].set(vectors[1])
        grid_vals = mix_last(
            flat_grid.reshape(item_count, planes, grid_len, 2 * grid_len), z_forward
        )
        grid_vals = mix_dim(grid_vals, cos_fwd, sin_fwd, "ky,bpyw->bpkw")
        grid_vals = real_space(
            lax.all_to_all(grid_vals, "ga", split_axis=2, concat_axis=1, tiled=True)
        )
        grid_vals = mix_dim(grid_vals, cos_back, sin_back, "ky,bpyw->bpkw")
        flat_grid = mix_last(grid_vals, z_backward).reshape(item_count, cell_count)
        return jnp.stack([flat_grid[:, slot_re], flat_grid[:, slot_im]])

    def contract(first_part, second_part):
        return jnp.einsum("pg,bg->pb", first_part, second_part, precision=top_precision)

    def spread(weights, proj_table):
        return jnp.einsum("pb,pg->bg", weights, proj_table, precision=top_precision)

    def projected_part(vectors):
        proj_re = contract(projectors[0], vectors[0]) + contract(projectors[1], vectors[1])
        proj_im = contract(projectors[0], vectors[1]) - contract(projectors[1], vectors[0])
        proj_re, proj_im = lax.psum((proj_re, proj_im), "ga")
        mixed_re = jnp.dot(
            coupling,
            proj_re / total_pw,
            precision=top_precision,
            preferred_element_type=jnp.float32,
        )
        mixed_im = jnp.dot(
            coupling,
            proj_im / total_pw,
            precision=top_precision,
            preferred_element_type=jnp.float32,
        )
        out_re = spread(mixed_re, projectors[0]) - spread(mixed_im, projectors[1])
        out_im = spread(mixed_re, projectors[1]) + spread(mixed_im, projectors[0])
        return jnp.stack([out_re, out_im])

    def apply_h(vectors):
        return kin_weight * vectors + local_part(vectors) + projected_part(vectors)

    def gram_sums(basis, pair_list):
        stacked = []
        for index_one, index_two, use_kin in pair_list:
            stacked.append(
                band_dot(basis[index_one], basis[index_two], kin_weight if use_kin else 1.0)
            )
        summed = lax.psum(jnp.stack(stacked), "ga") / total_pw
        found = {}
        for slot_num, entry in enumerate(pair_list):
            index_one, index_two, use_kin = entry
            found[use_kin, index_one, index_two] = summed[slot_num]
            found[use_kin, index_two, index_one] = summed[slot_num]
        return found

    def realize(coef_map, basis):
        running = jnp.zeros_like(basis[0])
        for index_one, coef_a in coef_map.items():
            running = (
                running
                + per_band(jnp.zeros((band_local,), jnp.float32) + coef_a) * basis[index_one]
            )
        return running

    h_zero = apply_h(coeffs)
    basis = [coeffs, h_zero]
    gram_table = gram_sums(basis, new_pairs(0, 2, (False, True)))
    psi_map = {0: 1.0}
    ham_map = {1: 1.0}
    eps_zero = gram_form(gram_table, psi_map, ham_map, False) / (
        gram_form(gram_table, psi_map, psi_map, False) + small_eps
    )
    r_map = combine([(1.0, ham_map), (-eps_zero, psi_map)])
    level_zero = gram_form(gram_table, r_map, r_map, True) / (
        gram_form(gram_table, r_map, r_map, False) + small_eps
    )
    p_zero = precondition(realize(r_map, basis), kinetic, level_zero)
    g_zero = apply_h(p_zero)
    basis = [coeffs, h_zero, p_zero, g_zero]
    gram_table.update(gram_sums(basis, new_pairs(2, 4, (False, True))))
    q_map = combine([(1.0, {3: 1.0}), (-eps_zero, {2: 1.0})])
    lam_zero = -gram_form(gram_table, r_map, q_map, False) / (
        gram_form(gram_table, q_map, q_map, False) + small_eps
    )
    psi_one_map = combine([(1.0, psi_map), (lam_zero, {2: 1.0})])
    h_one_map = combine([(1.0, ham_map), (lam_zero, {3: 1.0})])
    eps_one = gram_form(gram_table, psi_one_map, h_one_map, False) / (
        gram_form(gram_table, psi_one_map, psi_one_map, False) + small_eps
    )
    r_one_map = combine([(1.0, h_one_map), (-eps_one, psi_one_map)])
    change_map = combine([(1.0, r_map), (-1.0, r_one_map)])
    weight_one = gram_form(gram_table, r_map, change_map, False) / (
        gram_form(gram_table, change_map, change_map, False) + small_eps
    )
    step_mid = weight_one * lam_zero
    psi_mid_map = combine([(1.0, psi_map), (step_mid, {2: 1.0})])
    h_mid_map = combine([(1.0, ham_map), (step_mid, {3: 1.0})])
    r_mid_map = combine([(1.0, r_map), (-weight_one, change_map)])
    eps_mid = gram_form(gram_table, psi_mid_map, h_mid_map, False) / (
        gram_form(gram_table, psi_mid_map, psi_mid_map, False) + small_eps
    )
    level_mid = gram_form(gram_table, r_mid_map, r_mid_map, True) / (
        gram_form(gram_table, r_mid_map, r_mid_map, False) + small_eps
    )
    p_one = precondition(realize(r_mid_map, basis), kinetic, level_mid)
    g_one = apply_h(p_one)
    basis = [coeffs, h_zero, p_zero, g_zero, p_one, g_one]
    gram_table.update(gram_sums(basis, new_pairs(4, 6, (False,))))
    q_one_map = combine([(1.0, {5: 1.0}), (-eps_mid, {4: 1.0})])
    lam_one = -gram_form(gram_table, r_mid_map, q_one_map, False) / (
        gram_form(gram_table, q_one_map, q_one_map, False) + small_eps
    )
    new_map = combine([(1.0, psi_mid_map), (lam_one, {4: 1.0})])
    ham_new_map = combine([(1.0, h_mid_map), (lam_one, {5: 1.0})])
    norm_new = gram_form(gram_table, new_map, new_map, False) + small_eps
    energy = gram_form(gram_table, new_map, ham_new_map, False) / norm_new
    resid_map = combine([(1.0, ham_new_map), (-energy, new_map)])
    residual_norm = gram_form(gram_table, resid_map, resid_map, False) / norm_new
    new_bands = realize(new_map, basis)
    new_ham = realize(ham_new_map, basis)
    blank_rows = jnp.zeros((2, band_local, band_local * lax.axis_size("band")), jnp.float32)
    first_row = jnp.int32(0)
    over_rows = blank_rows
    ham_rows = blank_rows
    piece_bands = lax.all_gather(new_bands, "band", axis=1, tiled=True)
    piece_ham = lax.all_gather(new_ham, "band", axis=1, tiled=True)
    over_rows = lax.dynamic_update_slice_in_dim(
        over_rows, pair_products(new_bands, piece_bands), first_row, 2
    )
    ham_rows = lax.dynamic_update_slice_in_dim(
        ham_rows, pair_products(new_bands, piece_ham), first_row, 2
    )
    over_rows, ham_rows = (over_rows, ham_rows)
    over_rows, ham_rows = lax.psum((over_rows, ham_rows), "ga")
    correlation = over_rows / total_pw
    subspace = ham_rows / total_pw
    return (new_bands, energy, residual_norm, correlation, subspace)


QUAD = 4
TRIPLE = 3
MESH = pl.DeviceIdType.MESH


def split_const(values):
    high = np.asarray(values, np.float32).astype(jnp.bfloat16)
    low = (values - high.astype(np.float64)).astype(np.float32).astype(jnp.bfloat16)
    return np.stack([high, low])


def const_tables(grid_len, group):
    planes = grid_len // group
    chunks = planes // QUAD
    unit = 2.0 * np.pi / grid_len
    quarter = grid_len / 4.0
    chunk = np.arange(chunks)[:, None, None, None]
    dev = np.arange(group)[None, :, None, None]
    part = np.arange(2)[None, None, :, None]
    inner = np.arange(QUAD)[None, None, None, :]
    y_real = (dev * planes + chunk * QUAD + inner + 0 * part).reshape(-1)
    part_row = (part + 0 * (dev + chunk + inner)).reshape(-1)
    freq = np.arange(grid_len)
    phase = (y_real[:, None] * freq[None, :]) % grid_len
    tab_a = np.cos(unit * (phase - quarter * part_row[:, None]))
    tab_b = np.cos(unit * (phase + quarter * (1 - part_row[:, None])))
    wave = split_const(np.concatenate([tab_a, tab_b], axis=0))
    four = np.repeat(np.arange(4), grid_len)
    zed = np.tile(freq, 4)
    theta = 2.0 * np.pi * ((four[:, None] * four[None, :] % 4) / 4.0
                           + (zed[:, None] * zed[None, :] % grid_len) / grid_len)
    fourz = split_const(np.concatenate([np.cos(theta), np.sin(theta)], axis=1))
    dft = 2.0 * np.pi * np.outer(np.arange(group), np.arange(group)) / group
    real_mix = np.zeros((group, 2, QUAD, group, 2, QUAD))
    for row in range(QUAD):
        real_mix[:, 0, row, :, 0, row] = np.cos(dft)
        real_mix[:, 1, row, :, 1, row] = np.cos(dft)
        real_mix[:, 0, row, :, 1, row] = -np.sin(dft)
        real_mix[:, 1, row, :, 0, row] = np.sin(dft)
    size = group * 2 * QUAD
    real_mix = real_mix.reshape(size, size)

    def stacked(mat):
        high, low = split_const(mat)
        return np.concatenate([high, high, low], axis=1)

    across = np.stack([stacked(real_mix), stacked(real_mix.T)])
    b_lane = np.repeat(np.arange(TRIPLE), 4 * grid_len)
    a_lane = np.tile(np.repeat(np.arange(4), grid_len), TRIPLE)
    one = 2.0 * np.pi * (a_lane * b_lane) / planes
    two = unit * np.outer(np.arange(group), TRIPLE * a_lane + b_lane)
    lane_tw = np.stack([np.cos(one), np.sin(one)]).astype(np.float32)[:, None, :]
    dev_tw = np.stack([np.cos(two), np.sin(two)]).astype(np.float32)[:, :, None, :]
    return wave, fourz, across, lane_tw, dev_tw


def two_parts(values):
    high = values.astype(jnp.bfloat16)
    low = (values - high.astype(jnp.float32)).astype(jnp.bfloat16)
    return high, low


def bdot(left, right):
    return jnp.dot(left, right, preferred_element_type=jnp.float32)


def sweep_kernel(
    dims,
    coeffs_ref, cell_ref, potential_hbm, proj_hbm, strength_ref, atom_ref, chan_ref,
    wave_ref, fourz_hbm, across_ref, lane_ref, dev_ref,
    new_ref, scal_ref,
    hot_ref, hot_t_ref, ta_ref, tb_ref, key_ref, pot_ref, potential_ref, proj_ref, fourz_ref, in_sem,
    fsend, frecv, bsend, brecv, psend, precv, gsend, grecv, nsend, nrecv, isend, irecv, lsend, lrecv, csend, crecv,
    fs_sem, fr_sem, bs_sem, br_sem, ps_sem, pr_sem, gs_sem, gr_sem, ns_sem, nr_sem, cs_sem, cr_sem,
):
    group, bands, chunks, grid_len, total_pw, pw = dims
    rows = group * 2 * QUAD
    lanes = TRIPLE * 4 * grid_len
    quad_lanes = 4 * grid_len
    me = lax.axis_index("ga")
    band = lax.axis_index("band")

    loads = [
        pltpu.make_async_copy(source, target, in_sem.at[k])
        for k, (source, target) in enumerate(
            ((proj_hbm, proj_ref), (potential_hbm, potential_ref), (fourz_hbm, fourz_ref)))
    ]
    for load in loads:
        load.start()
    barrier = pltpu.get_barrier_semaphore()
    for off in range(1, group):
        pl.semaphore_signal(barrier, inc=1, device_id={"ga": lax.rem(me + off, group)}, device_id_type=MESH)
    for off in range(1, bands):
        pl.semaphore_signal(barrier, inc=1, device_id={"band": lax.rem(band + off, bands)}, device_id_type=MESH)

    def whole(values):
        return jnp.floor(values)

    cell = cell_ref[...].astype(jnp.float32)
    plane = whole((cell + 0.5) * (1.0 / (grid_len * grid_len)))
    in_plane = cell - plane * (grid_len * grid_len)
    y_num = whole((in_plane + 0.5) * (1.0 / grid_len))
    z_num = in_plane - y_num * grid_len
    key_ref[...] = plane * grid_len + z_num

    def signed(values):
        return jnp.where(2.0 * values < grid_len, values, values - grid_len)

    f_x = signed(plane * group + me.astype(jnp.float32))
    f_y, f_z = signed(y_num), signed(z_num)
    kin = kin_unit * (f_x * f_x + f_y * f_y + f_z * f_z)

    def build_hot(step, carry):
        at = pl.multiple_of(step * 128, 128)
        key_col = jnp.transpose(jnp.broadcast_to(key_ref[:, pl.ds(at, 128)], (128, 128)))
        lane_id = lax.broadcasted_iota(jnp.int32, (128, 128), 1).astype(jnp.float32)
        for k in range(lanes // 128):
            hit = jnp.where(lane_id == key_col - 128.0 * k, 1.0, 0.0)
            hot_ref[pl.ds(at, 128), k * 128:(k + 1) * 128] = hit.astype(jnp.bfloat16)
        return carry

    lax.fori_loop(0, pw // 128, build_hot, 0)
    y_hot = jnp.where(lax.broadcasted_iota(jnp.int32, (grid_len, pw), 0).astype(jnp.float32) == y_num, 1.0, 0.0).astype(jnp.bfloat16)
    for part in range(chunks):
        for table, base in ((ta_ref, 0), (tb_ref, chunks * rows)):
            at = base + part * rows
            table[part] = bdot(wave_ref[0, at:at + rows, :], y_hot) + bdot(wave_ref[1, at:at + rows, :], y_hot)

    def build_turn():
        turn_rows = 128

        def step_turn(step, carry):
            at = pl.multiple_of(step * turn_rows, turn_rows)
            row_id = (lax.broadcasted_iota(jnp.int32, (turn_rows, pw), 0) + at).astype(jnp.float32)
            hot_t_ref[pl.ds(at, turn_rows), :] = jnp.where(row_id == key_ref[...], 1.0, 0.0).astype(jnp.bfloat16)
            return carry

        lax.fori_loop(0, lanes // turn_rows, step_turn, 0)

    def build_potential():
        for part in range(chunks):
            for b in range(TRIPLE):
                for a in range(4):
                    at = (b * 4 + a) * grid_len
                    block = potential_ref[:, TRIPLE * a + b, part * QUAD:(part + 1) * QUAD, :] * (1.0 / grid_len**3)
                    pot_ref[part, :, :QUAD, at:at + grid_len] = block
                    pot_ref[part, :, QUAD:, at:at + grid_len] = block

    def build_coupling():
        atoms, chans = strength_ref.shape[0] // strength_ref.shape[1], strength_ref.shape[1]
        size = atoms * chans
        ident = atom_ref[...] * chans + chan_ref[...]
        hot = (lax.broadcasted_iota(jnp.int32, (size, ident.shape[1]), 0) == ident).astype(jnp.float32)
        row_at = lax.broadcasted_iota(jnp.int32, (size, size), 0)
        col_at = lax.broadcasted_iota(jnp.int32, (size, size), 1)
        tiled = jnp.concatenate([strength_ref[...]] * atoms, axis=1)
        same = (row_at // chans == col_at // chans).astype(jnp.float32)
        block = tiled * same
        block = 0.5 * (block + jnp.transpose(block))
        half = lax.dot_general(hot, block, (((0,), (0,)), ((), ())), precision=top_precision, preferred_element_type=jnp.float32)
        return jnp.dot(half, hot, precision=top_precision, preferred_element_type=jnp.float32)

    pl.semaphore_wait(barrier, group + bands - 2)

    sign = jnp.where(lax.broadcasted_iota(jnp.int32, (1, 2 * QUAD, 1), 1) < QUAD, -1.0, 1.0).astype(jnp.float32)

    def times_i(values):
        return pltpu.roll(values, QUAD, 1) * sign

    def lane_split(values):
        return [values[..., k * quad_lanes:(k + 1) * quad_lanes] for k in range(TRIPLE)]

    def mix_fourz(triple, direction):
        stacked = jnp.concatenate([t.reshape(rows, quad_lanes) for t in triple], axis=0)
        high, low = two_parts(stacked)
        out = bdot(high, fourz_ref[0]) + bdot(low, fourz_ref[0]) + bdot(high, fourz_ref[1])
        out = out.reshape(TRIPLE * group, 2 * QUAD, 2 * quad_lanes)
        mixed = out[..., :quad_lanes] + direction * times_i(out[..., quad_lanes:])
        return [mixed[k * group:(k + 1) * group] for k in range(TRIPLE)]

    def turn_lane(triple, direction):
        done = [triple[0]]
        for k in range(1, TRIPLE):
            at = slice(k * quad_lanes, (k + 1) * quad_lanes)
            done.append(triple[k] * lane_ref[0, :, at][None] + direction * times_i(triple[k]) * lane_ref[1, :, at][None])
        return done

    def three(triple, direction):
        total = triple[1] + triple[2]
        diff = times_i(triple[1] - triple[2]) * (direction * 0.8660254037844386)
        base = triple[0] - 0.5 * total
        return [triple[0] + total, base + diff, base - diff]

    def turn_dev(values, direction):
        return values * dev_ref[0] + direction * times_i(values) * dev_ref[1]

    def mix_devices(values, which):
        high, low = two_parts(values.reshape(rows, lanes))
        return bdot(across_ref[which], jnp.concatenate([high, low, high], axis=0))

    def all_sum(local, send, recv, send_sem, recv_sem, shape_at):
        send[shape_at] = local
        recv[shape_at, me] = local
        for off in range(1, group):
            pltpu.make_async_remote_copy(
                src_ref=send.at[shape_at], dst_ref=recv.at[shape_at, me],
                send_sem=send_sem.at[shape_at, off - 1], recv_sem=recv_sem.at[shape_at, off - 1],
                device_id={"ga": lax.rem(me + off, group)}, device_id_type=MESH).start()

    def all_sum_end(send, recv, send_sem, recv_sem, shape_at):
        for off in range(1, group):
            pltpu.make_async_remote_copy(
                src_ref=send.at[shape_at], dst_ref=recv.at[shape_at, lax.rem(me + group - off, group)],
                send_sem=send_sem.at[shape_at, off - 1], recv_sem=recv_sem.at[shape_at, off - 1],
                device_id={"ga": lax.rem(me + off, group)}, device_id_type=MESH).wait()
        running = recv[shape_at, 0]
        for dev in range(1, group):
            running = running + recv[shape_at, dev]
        return running

    def piece(turn, part, off, send, recv, send_sem, recv_sem, incoming):
        peer = lax.rem(me + off, group)
        source = lax.rem(me + group - off, group) if incoming else me
        return pltpu.make_async_remote_copy(
            src_ref=send.at[turn, part, peer], dst_ref=recv.at[turn, part, source],
            send_sem=send_sem.at[turn, part, off - 1], recv_sem=recv_sem.at[turn, part, off - 1],
            device_id={"ga": peer}, device_id_type=MESH)

    def apply_h(turn, vector):
        v_re, v_im = vector[0:1], vector[1:2]
        fwd = (fsend, frecv, fs_sem, fr_sem)
        back = (bsend, brecv, bs_sem, br_sem)

        def put(part, carry):
            high, low = two_parts(ta_ref[part] * v_re + tb_ref[part] * v_im)
            out = bdot(jnp.concatenate([high, low], axis=0), hot_ref[...])
            out = (out[:rows] + out[rows:]).reshape(group, 2 * QUAD, lanes)
            fsend[turn, part] = out
            frecv[turn, part, me] = fsend[turn, part, me]
            for off in range(1, group):
                piece(turn, part, off, *fwd, False).start()
            return carry

        lax.fori_loop(0, chunks, put, 0)
        if turn == 0:
            for load in loads:
                load.wait()
        sums = lax.dot_general(vector, proj_ref[...], (((1,), (1,)), ((), ())), precision=top_precision, preferred_element_type=jnp.float32)
        all_sum(sums, psend, precv, ps_sem, pr_sem, turn)
        if turn == 0:
            build_potential()
            shared.append(build_coupling())
            build_turn()

        def middle(part, carry):
            for off in range(1, group):
                piece(turn, part, off, *fwd, True).wait()
            triple = turn_lane(three(lane_split(frecv[turn, part]), 1.0), 1.0)
            values = turn_dev(jnp.concatenate(mix_fourz(triple, 1.0), axis=-1), 1.0)
            values = mix_devices(values, 0) * pot_ref[part].reshape(rows, lanes)
            values = mix_devices(values, 1).reshape(group, 2 * QUAD, lanes)
            triple = mix_fourz(lane_split(turn_dev(values, -1.0)), -1.0)
            triple = three(turn_lane(triple, -1.0), -1.0)
            bsend[turn, part] = jnp.concatenate(triple, axis=-1)
            brecv[turn, part, me] = bsend[turn, part, me]
            for off in range(1, group):
                piece(turn, part, off, *back, False).start()
            return carry

        lax.fori_loop(0, chunks, middle, 0)
        sums = all_sum_end(psend, precv, ps_sem, pr_sem, turn) * (1.0 / total_pw)
        half = sums.shape[1] // 2
        pair = jnp.concatenate([
            sums[0:1, :half] + sums[1:2, half:], sums[1:2, :half] - sums[0:1, half:]], axis=0)
        mixed = jnp.dot(pair, shared[0], precision=top_precision, preferred_element_type=jnp.float32)
        m_re, m_im = mixed[0:1], mixed[1:2]
        weights = jnp.concatenate([
            jnp.concatenate([m_re, -m_im], axis=1), jnp.concatenate([m_im, m_re], axis=1)], axis=0)
        nonlocal_part = jnp.dot(weights, proj_ref[...], precision=top_precision, preferred_element_type=jnp.float32)
        start = kin * vector + nonlocal_part

        def take(part, carry):
            run_re, run_im = carry
            for off in range(1, group):
                piece(turn, part, off, *back, True).wait()
            high, low = two_parts(brecv[turn, part].reshape(rows, lanes))
            out = bdot(jnp.concatenate([high, low], axis=0), hot_t_ref[...])
            out = out[:rows] + out[rows:]
            run_re = run_re + jnp.sum(ta_ref[part] * out, axis=0, keepdims=True)
            run_im = run_im + jnp.sum(tb_ref[part] * out, axis=0, keepdims=True)
            return run_re, run_im

        run_re, run_im = lax.fori_loop(0, chunks, take, (start[0:1], start[1:2]))
        return jnp.concatenate([run_re, run_im], axis=0)

    def as_row(values):
        total = jnp.sum(jnp.sum(values, axis=0, keepdims=True), axis=1, keepdims=True)
        return jnp.broadcast_to(total, (1, 128))

    row_count = gsend.shape[1]

    def gram_sums(turn, basis, pair_list):
        found_rows = []
        for one, two, use_kin in pair_list:
            product = basis[one] * basis[two]
            found_rows.append(as_row(product * kin if use_kin else product))
        found_rows += [jnp.zeros((1, 128), jnp.float32)] * (row_count - len(found_rows))
        all_sum(jnp.concatenate(found_rows, axis=0), gsend, grecv, gs_sem, gr_sem, turn)
        summed = all_sum_end(gsend, grecv, gs_sem, gr_sem, turn) * (1.0 / total_pw)
        found = {}
        for slot, (one, two, use_kin) in enumerate(pair_list):
            value = summed[slot:slot + 1]
            found[use_kin, one, two] = value
            found[use_kin, two, one] = value
        return found

    def realize(coef_map, basis):
        running = 0.0
        for index, coef in coef_map.items():
            running = running + (basis[index] if isinstance(coef, float) and coef == 1.0 else spread_row(coef) * basis[index])
        return running

    def spread_row(coef):
        return coef if isinstance(coef, float) else coef[:, 0:1]

    def smooth(residual, level):
        ratio = kin / (1.5 * level[:, 0:1] + 1.0)
        poly = 27.0 + ratio * (18.0 + ratio * (12.0 + 8.0 * ratio))
        square = ratio * ratio
        return residual * (poly / (poly + 16.0 * square * square))

    shared = []
    coeffs = coeffs_ref[:, 0, :]
    h_zero = apply_h(0, coeffs)
    basis = [coeffs, h_zero]
    gram = gram_sums(0, basis, new_pairs(0, 2, (False, True)))
    psi = {0: 1.0}
    ham = {1: 1.0}
    eps_zero = gram_form(gram, psi, ham, False) / (gram_form(gram, psi, psi, False) + small_eps)
    r_map = combine([(1.0, ham), (-eps_zero, psi)])
    level = gram_form(gram, r_map, r_map, True) / (gram_form(gram, r_map, r_map, False) + small_eps)
    p_zero = smooth(realize(r_map, basis), level)
    g_zero = apply_h(1, p_zero)
    basis += [p_zero, g_zero]
    gram.update(gram_sums(1, basis, new_pairs(2, 4, (False, True))))
    q_map = combine([(1.0, {3: 1.0}), (-eps_zero, {2: 1.0})])
    lam_zero = -gram_form(gram, r_map, q_map, False) / (gram_form(gram, q_map, q_map, False) + small_eps)
    psi_one = combine([(1.0, psi), (lam_zero, {2: 1.0})])
    h_one = combine([(1.0, ham), (lam_zero, {3: 1.0})])
    eps_one = gram_form(gram, psi_one, h_one, False) / (gram_form(gram, psi_one, psi_one, False) + small_eps)
    r_one = combine([(1.0, h_one), (-eps_one, psi_one)])
    change = combine([(1.0, r_map), (-1.0, r_one)])
    weight = gram_form(gram, r_map, change, False) / (gram_form(gram, change, change, False) + small_eps)
    step = weight * lam_zero
    psi_mid = combine([(1.0, psi), (step, {2: 1.0})])
    h_mid = combine([(1.0, ham), (step, {3: 1.0})])
    r_mid = combine([(1.0, r_map), (-weight, change)])
    eps_mid = gram_form(gram, psi_mid, h_mid, False) / (gram_form(gram, psi_mid, psi_mid, False) + small_eps)
    level = gram_form(gram, r_mid, r_mid, True) / (gram_form(gram, r_mid, r_mid, False) + small_eps)
    p_one = smooth(realize(r_mid, basis), level)

    def swap(which, send, recv, off, incoming):
        source = lax.rem(band + bands - off, bands) if incoming else band
        return pltpu.make_async_remote_copy(
            src_ref=send, dst_ref=recv.at[source],
            send_sem=ns_sem.at[which, off - 1], recv_sem=nr_sem.at[which, off - 1],
            device_id={"band": lax.rem(band + off, bands)}, device_id_type=MESH)

    def share(which, send, recv, values):
        send[...] = values
        recv[band] = values
        for off in range(1, bands):
            swap(which, send, recv, off, False).start()

    share(0, nsend, nrecv, jnp.stack([realize(psi_mid, basis), p_one, realize(h_mid, basis)]))
    g_one = apply_h(2, p_one)
    share(1, isend, irecv, g_one)
    basis += [p_one, g_one]
    gram.update(gram_sums(2, basis, new_pairs(4, 6, (False,))))
    q_one = combine([(1.0, {5: 1.0}), (-eps_mid, {4: 1.0})])
    lam_one = -gram_form(gram, r_mid, q_one, False) / (gram_form(gram, q_one, q_one, False) + small_eps)
    new_map = combine([(1.0, psi_mid), (lam_one, {4: 1.0})])
    ham_new = combine([(1.0, h_mid), (lam_one, {5: 1.0})])
    norm_new = gram_form(gram, new_map, new_map, False) + small_eps
    energy = gram_form(gram, new_map, ham_new, False) / norm_new
    resid = combine([(1.0, ham_new), (-energy, new_map)])
    resid_norm = gram_form(gram, resid, resid, False) / norm_new
    new = realize(new_map, basis)
    new_h = realize(ham_new, basis)
    new_ref[...] = new
    share(2, lsend, lrecv, jnp.broadcast_to(lam_one, (8, 128)))
    for which, send, recv in ((0, nsend, nrecv), (1, isend, irecv), (2, lsend, lrecv)):
        for off in range(1, bands):
            swap(which, send, recv, off, True).wait()
    found_rows = []
    others = []
    for other in range(bands):
        lam = lrecv[other, 0:1, 0:1]
        others.append((nrecv[other, 0] + lam * nrecv[other, 1], nrecv[other, 2] + lam * irecv[other]))
    for first in (0, 1):
        for imag in (False, True):
            for other in range(bands):
                o_re = others[other][first][0:1]
                o_im = others[other][first][1:2]
                if imag:
                    found_rows.append(as_row(new[0:1] * o_im - new[1:2] * o_re))
                else:
                    found_rows.append(as_row(new[0:1] * o_re + new[1:2] * o_im))
    all_sum(jnp.concatenate(found_rows, axis=0), csend, crecv, cs_sem, cr_sem, 0)
    summed = all_sum_end(csend, crecv, cs_sem, cr_sem, 0) * (1.0 / total_pw)
    scal_ref[...] = jnp.concatenate([summed, energy, resid_norm, jnp.zeros((6, 128), jnp.float32)], axis=0)


def finish_kernel(bands, new_ref, scal_ref, bands_ref, energy_ref, norm_ref, corr_ref, sub_ref):
    bands_ref[:, 0, :] = new_ref[...]
    lane = lax.broadcasted_iota(jnp.int32, (1, bands), 1)
    for ref, base in ((corr_ref, 0), (sub_ref, 2 * bands)):
        for part in range(2):
            row = jnp.zeros((1, bands), jnp.float32)
            for other in range(bands):
                at = base + part * bands + other
                row = jnp.where(lane == other, scal_ref[at:at + 1, :bands], row)
            ref[part] = row
    energy_ref[0] = scal_ref[4 * bands, 0]
    norm_ref[0] = scal_ref[4 * bands + 1, 0]


def kernel_body(coeffs, cell_map, potential, projectors, strengths, proj_atom, proj_chan):
    group = lax.axis_size("ga")
    bands = lax.axis_size("band")
    grid_len = potential.shape[0]
    planes = grid_len // group
    chunks = planes // QUAD
    pw = coeffs.shape[2]
    total_pw = pw * group
    rows = group * 2 * QUAD
    lanes = planes * grid_len
    proj_rows = 2 * projectors.shape[1]
    tables = [jnp.asarray(t) for t in const_tables(grid_len, group)]
    gram_rows = 16
    piece_shape = (3, chunks, group, 2 * QUAD, lanes)
    dma = pltpu.SemaphoreType.DMA
    vmem = pl.BlockSpec(memory_space=pltpu.VMEM)
    far = pl.BlockSpec(memory_space=pl.ANY)
    f32 = jnp.float32
    new, scal = pl.pallas_call(
        functools.partial(sweep_kernel, (group, bands, chunks, grid_len, total_pw, pw)),
        out_shape=(
            jax.ShapeDtypeStruct((2, pw), f32),
            jax.ShapeDtypeStruct((4 * bands + 8, 128), f32),
        ),
        in_specs=[vmem, vmem, far, far] + [vmem] * 4 + [far] + [vmem] * 3,
        out_specs=(vmem, vmem),
        scratch_shapes=[
            pltpu.VMEM((pw, lanes), jnp.bfloat16),
            pltpu.VMEM((lanes, pw), jnp.bfloat16),
            pltpu.VMEM((chunks, rows, pw), f32),
            pltpu.VMEM((chunks, rows, pw), f32),
            pltpu.VMEM((1, pw), f32),
            pltpu.VMEM((chunks, group, 2 * QUAD, lanes), f32),
            pltpu.VMEM((group, planes, planes, grid_len), f32),
            pltpu.VMEM((proj_rows, pw), f32),
            pltpu.VMEM(tables[1].shape, jnp.bfloat16),
            pltpu.SemaphoreType.DMA((3,)),
            pltpu.VMEM(piece_shape, f32),
            pltpu.VMEM(piece_shape, f32),
            pltpu.VMEM(piece_shape, f32),
            pltpu.VMEM(piece_shape, f32),
            pltpu.VMEM((3, 2, proj_rows), f32),
            pltpu.VMEM((3, group, 2, proj_rows), f32),
            pltpu.VMEM((3, gram_rows, 128), f32),
            pltpu.VMEM((3, group, gram_rows, 128), f32),
            pltpu.VMEM((3, 2, pw), f32),
            pltpu.VMEM((bands, 3, 2, pw), f32),
            pltpu.VMEM((2, pw), f32),
            pltpu.VMEM((bands, 2, pw), f32),
            pltpu.VMEM((8, 128), f32),
            pltpu.VMEM((bands, 8, 128), f32),
            pltpu.VMEM((1, 4 * bands, 128), f32),
            pltpu.VMEM((1, group, 4 * bands, 128), f32),
            dma((3, chunks, group - 1)), dma((3, chunks, group - 1)),
            dma((3, chunks, group - 1)), dma((3, chunks, group - 1)),
            dma((3, group - 1)), dma((3, group - 1)),
            dma((3, group - 1)), dma((3, group - 1)),
            dma((3, bands - 1)), dma((3, bands - 1)),
            dma((1, group - 1)), dma((1, group - 1)),
        ],
        compiler_params=pltpu.CompilerParams(
            collective_id=0, has_side_effects=True, vmem_limit_bytes=60 * 1024 * 1024
        ),
        name="sweeps",
    )(
        coeffs, cell_map.reshape(1, pw), potential.reshape(group, planes, planes, grid_len),
        projectors.reshape(proj_rows, pw), strengths.reshape(-1, strengths.shape[2]),
        proj_atom.reshape(1, -1), proj_chan.reshape(1, -1), *tables,
    )

    smem = pl.BlockSpec(memory_space=pltpu.SMEM)
    return pl.pallas_call(
        functools.partial(finish_kernel, bands),
        out_shape=(
            jax.ShapeDtypeStruct((2, 1, pw), f32),
            jax.ShapeDtypeStruct((1,), f32),
            jax.ShapeDtypeStruct((1,), f32),
            jax.ShapeDtypeStruct((2, 1, bands), f32),
            jax.ShapeDtypeStruct((2, 1, bands), f32),
        ),
        in_specs=[vmem, vmem],
        out_specs=(vmem, smem, smem, vmem, vmem),
        name="finish",
    )(new, scal)


def body(coeffs, cell_map, potential, projectors, strengths, proj_atom, proj_chan):
    group = lax.axis_size("ga")
    grid_len = potential.shape[0]
    planes = grid_len // group
    fits = (
        planes == 4 * TRIPLE
        and 4 * grid_len % 128 == 0
        and coeffs.shape[1] == 1
        and coeffs.shape[2] % 256 == 0
        and 2 * projectors.shape[1] == 128
    )
    chosen = kernel_body if fits else plain_body
    return chosen(coeffs, cell_map, potential, projectors, strengths, proj_atom, proj_chan)


def solution(mesh):
    placed = (
        P(None, "band", "ga"),
        P("ga"),
        P(None, "ga", None),
        P(None, None, "ga"),
        P(),
        P(),
        P(),
    )
    return jax.shard_map(
        body,
        mesh=mesh,
        in_specs=placed,
        out_specs=(
            P(None, "band", "ga"),
            P("band"),
            P("band"),
            P(None, "band", None),
            P(None, "band", None),
        ),
        check_vma=False,
    )
```

profile of v0, /device:TPU:0, one launch (start us, length us, event | category | flops | bytes accessed | tf_op | source)
XLA Modules:
  0.0 104.4 jit_solution(2413052306142160144)
XLA Ops:
  0.6 1.3 %reshape.28.cell_ref = s32[1,2304]{1,0:T(1,128)} reshape(s32[2304]{0:T(1024)} %param.13) | data formatting | bytes 18432 | tf_op jit(solution)/shard_map/reshape | solution.py:792
  1.9 2.3 %copy.17 = f32[96,12,96]{2,1,0:T(8,128)} copy(f32[96,12,96]{2,0,1:T(8,128)} %param.14) | data formatting | bytes 884736 | tf_op args[2]
  4.2 98.6 %sweeps.1 = (f32[2,2304]{1,0:T(2,128)}, f32[24,128]{1,0:T(8,128)}) custom-call(f32[2,1,2304]{2,1,0:T(1,128)} %coeffs_ref.1, s32[1,2304]{1,0:T(1,128)} %reshape.28.cell_ref, f32[8,12,12,96]{3,2,1,0:T(8,128)} %bitcast.5, f32[128,2304]{1,0:T(8,128)} %bitcast.6, f32[64,8]{1,0:T(8,128)} %bitcast.7, s32[1,64]{1,0:T(1,128)} %bitcast.8, s32[1,64]{1,0:T(1,128)} %bitcast.9, ...), custom_call_target="tpu_custom_call" | custom-call | tf_op jit(solution)/shard_map/sweeps/pallas_call | solution.py:745
  102.9 1.4 %finish.1 = (f32[2,1,2304]{2,1,0:T(1,128)}, f32[1]{0:T(128)}, f32[1]{0:T(128)}, f32[2,1,4]{2,1,0:T(1,128)}, f32[2,1,4]{2,1,0:T(1,128)}) custom-call(f32[2,2304]{1,0:T(2,128)} %get-tuple-element.7.new_ref, f32[24,128]{1,0:T(8,128)} %get-tuple-element.8.scal_ref), custom_call_target="tpu_custom_call" | custom-call | tf_op jit(solution)/shard_map/finish/pallas_call | solution.py:798
where the time goes:
time: 105 us; the launch traced here: 104 us
  Pallas kernels  100 us (95%)
  local copies, waits for them, and re-layouts  3.61 us (3%)
    pallas_call x1, Pallas kernels, kernel_body(): pl.pallas_call(functools.partial(sweep_kernel, (group, bands, chunks, gri...  98.6 us
    unnamed x1, local copies, waits for them, and re-layouts  2.3 us

commit v1 on v0

--- a/solution.py
+++ b/solution.py
@@ -299,6 +299,7 @@
 
 QUAD = 4
 TRIPLE = 3
+WIDE = 256
 MESH = pl.DeviceIdType.MESH
 
 
@@ -313,17 +314,18 @@
     chunks = planes // QUAD
     unit = 2.0 * np.pi / grid_len
     quarter = grid_len / 4.0
-    chunk = np.arange(chunks)[:, None, None, None]
-    dev = np.arange(group)[None, :, None, None]
+    dev = np.arange(group)[:, None, None, None]
+    chunk = np.arange(chunks)[None, :, None, None]
     part = np.arange(2)[None, None, :, None]
     inner = np.arange(QUAD)[None, None, None, :]
-    y_real = (dev * planes + chunk * QUAD + inner + 0 * part).reshape(-1)
-    part_row = (part + 0 * (dev + chunk + inner)).reshape(-1)
+    y_real = (dev * planes + chunk * QUAD + inner + 0 * part).reshape(group, -1)
+    part_row = (part + 0 * (dev + chunk + inner)).reshape(group, -1)
     freq = np.arange(grid_len)
-    phase = (y_real[:, None] * freq[None, :]) % grid_len
-    tab_a = np.cos(unit * (phase - quarter * part_row[:, None]))
-    tab_b = np.cos(unit * (phase + quarter * (1 - part_row[:, None])))
-    wave = split_const(np.concatenate([tab_a, tab_b], axis=0))
+    phase = (y_real[..., None] * freq) % grid_len
+    tab_a = np.cos(unit * (phase - quarter * part_row[..., None]))
+    tab_b = np.cos(unit * (phase + quarter * (1 - part_row[..., None])))
+    high, low = split_const(np.concatenate([tab_a, tab_b], axis=1))
+    wave = np.concatenate([high, low], axis=2)
     four = np.repeat(np.arange(4), grid_len)
     zed = np.tile(freq, 4)
     theta = 2.0 * np.pi * ((four[:, None] * four[None, :] % 4) / 4.0
@@ -359,8 +361,21 @@
     return high, low
 
 
+def split_rows(values):
+    high = values.astype(jnp.bfloat16).astype(jnp.float32)
+    return jnp.concatenate([high, values - high], axis=0).astype(jnp.bfloat16)
+
+
 def bdot(left, right):
     return jnp.dot(left, right, preferred_element_type=jnp.float32)
+
+
+def bdot_t(left, right):
+    return lax.dot_general(left, right, (((1,), (1,)), ((), ())), preferred_element_type=jnp.float32)
+
+
+def total_of(values):
+    return jnp.sum(jnp.sum(values, axis=0, keepdims=True), axis=1, keepdims=True)
 
 
 def sweep_kernel(
@@ -368,16 +383,26 @@
     coeffs_ref, cell_ref, potential_hbm, proj_hbm, strength_ref, atom_ref, chan_ref,
     wave_ref, fourz_hbm, across_ref, lane_ref, dev_ref,
     new_ref, scal_ref,
-    hot_ref, hot_t_ref, ta_ref, tb_ref, key_ref, pot_ref, potential_ref, proj_ref, fourz_ref, in_sem,
-    fsend, frecv, bsend, brecv, psend, precv, gsend, grecv, nsend, nrecv, isend, irecv, lsend, lrecv, csend, crecv,
-    fs_sem, fr_sem, bs_sem, br_sem, ps_sem, pr_sem, gs_sem, gr_sem, ns_sem, nr_sem, cs_sem, cr_sem,
+    hot_ref, mask_ref, group_ref, ta_ref, tb_ref, kin_ref, field_ref, back_ref,
+    pot_ref, potential_ref, proj_ref, fourz_ref, couple_ref, in_vec, out_vec, save_ref, in_sem,
+    ksend, krecv, xsend, xrecv, rsend, rrecv, hsend, hrecv, psend, precv,
+    gsend, grecv, nsend, nrecv, isend, irecv, lsend, lrecv, csend, crecv,
+    ks_sem, kr_sem, xs_sem, xr_sem, rs_sem, rr_sem, hs_sem, hr_sem, ps_sem, pr_sem,
+    gs_sem, gr_sem, ns_sem, nr_sem, cs_sem, cr_sem,
 ):
     group, bands, chunks, grid_len, total_pw, pw = dims
     rows = group * 2 * QUAD
+    slab = chunks * 2 * QUAD
     lanes = TRIPLE * 4 * grid_len
     quad_lanes = 4 * grid_len
+    folds = -(-lanes // WIDE)
+    tiles = pw // 128
     me = lax.axis_index("ga")
     band = lax.axis_index("band")
+    sides = [1 - 2 * lax.rem(me // (1 << bit), 2) for bit in range(3)]
+
+    def peer_of(mask):
+        return me + sum((sides[bit] << bit) if mask >> bit & 1 else 0 for bit in range(3))
 
     loads = [
         pltpu.make_async_copy(source, target, in_sem.at[k])
@@ -387,63 +412,90 @@
     for load in loads:
         load.start()
     barrier = pltpu.get_barrier_semaphore()
-    for off in range(1, group):
-        pl.semaphore_signal(barrier, inc=1, device_id={"ga": lax.rem(me + off, group)}, device_id_type=MESH)
+    for mask in range(1, group):
+        pl.semaphore_signal(barrier, inc=1, device_id={"ga": peer_of(mask)}, device_id_type=MESH)
     for off in range(1, bands):
         pl.semaphore_signal(barrier, inc=1, device_id={"band": lax.rem(band + off, bands)}, device_id_type=MESH)
 
+    cell = cell_ref[...].astype(jnp.float32)
+    for k in range(tiles):
+        ksend[:, k * 128:(k + 1) * 128] = cell[k:k + 1]
+    xsend[...] = coeffs_ref[:, 0, :]
+
+    far_first = (6, 7, 4, 5, 2, 3, 1)
+
+    def spread_copy(mask, send, recv, send_sem, recv_sem, incoming):
+        peer = peer_of(mask)
+        return pltpu.make_async_remote_copy(
+            src_ref=send, dst_ref=recv.at[peer if incoming else me],
+            send_sem=send_sem.at[mask - 1], recv_sem=recv_sem.at[mask - 1],
+            device_id={"ga": peer}, device_id_type=MESH)
+
+    def spread_start(send, recv, send_sem, recv_sem):
+        for mask in far_first:
+            spread_copy(mask, send, recv, send_sem, recv_sem, False).start()
+
+    def spread_wait(send, recv, send_sem, recv_sem):
+        for mask in range(1, group):
+            spread_copy(mask, send, recv, send_sem, recv_sem, True).wait()
+
+    keys = (ksend, krecv, ks_sem, kr_sem)
+    firsts = (xsend, xrecv, xs_sem, xr_sem)
+    pl.semaphore_wait(barrier, group + bands - 2)
+    spread_start(*keys)
+    spread_start(*firsts)
+    krecv[me] = ksend[...]
+    xrecv[me] = xsend[...]
+
     def whole(values):
         return jnp.floor(values)
 
-    cell = cell_ref[...].astype(jnp.float32)
-    plane = whole((cell + 0.5) * (1.0 / (grid_len * grid_len)))
-    in_plane = cell - plane * (grid_len * grid_len)
-    y_num = whole((in_plane + 0.5) * (1.0 / grid_len))
-    z_num = in_plane - y_num * grid_len
-    key_ref[...] = plane * grid_len + z_num
-
     def signed(values):
         return jnp.where(2.0 * values < grid_len, values, values - grid_len)
 
-    f_x = signed(plane * group + me.astype(jnp.float32))
-    f_y, f_z = signed(y_num), signed(z_num)
-    kin = kin_unit * (f_x * f_x + f_y * f_y + f_z * f_z)
-
-    def build_hot(step, carry):
-        at = pl.multiple_of(step * 128, 128)
-        key_col = jnp.transpose(jnp.broadcast_to(key_ref[:, pl.ds(at, 128)], (128, 128)))
-        lane_id = lax.broadcasted_iota(jnp.int32, (128, 128), 1).astype(jnp.float32)
-        for k in range(lanes // 128):
-            hit = jnp.where(lane_id == key_col - 128.0 * k, 1.0, 0.0)
-            hot_ref[pl.ds(at, 128), k * 128:(k + 1) * 128] = hit.astype(jnp.bfloat16)
-        return carry
-
-    lax.fori_loop(0, pw // 128, build_hot, 0)
-    y_hot = jnp.where(lax.broadcasted_iota(jnp.int32, (grid_len, pw), 0).astype(jnp.float32) == y_num, 1.0, 0.0).astype(jnp.bfloat16)
-    for part in range(chunks):
-        for table, base in ((ta_ref, 0), (tb_ref, chunks * rows)):
-            at = base + part * rows
-            table[part] = bdot(wave_ref[0, at:at + rows, :], y_hot) + bdot(wave_ref[1, at:at + rows, :], y_hot)
-
-    def build_turn():
-        turn_rows = 128
-
-        def step_turn(step, carry):
-            at = pl.multiple_of(step * turn_rows, turn_rows)
-            row_id = (lax.broadcasted_iota(jnp.int32, (turn_rows, pw), 0) + at).astype(jnp.float32)
-            hot_t_ref[pl.ds(at, turn_rows), :] = jnp.where(row_id == key_ref[...], 1.0, 0.0).astype(jnp.bfloat16)
-            return carry
-
-        lax.fori_loop(0, lanes // turn_rows, step_turn, 0)
+    def numbers(cells):
+        plane = whole((cells + 0.5) * (1.0 / (grid_len * grid_len)))
+        in_plane = cells - plane * (grid_len * grid_len)
+        y_num = whole((in_plane + 0.5) * (1.0 / grid_len))
+        return plane, y_num, in_plane - y_num * grid_len
+
+    def kinetic(plane, y_num, z_num, device):
+        f_x = signed(plane * group + device)
+        f_y, f_z = signed(y_num), signed(z_num)
+        return kin_unit * (f_x * f_x + f_y * f_y + f_z * f_z)
+
+    def marks(numbers_row, count):
+        wide_row = jnp.broadcast_to(numbers_row, (16, pw)).astype(jnp.bfloat16)
+        row_id = lax.broadcasted_iota(jnp.int32, (16, pw), 0).astype(jnp.float32).astype(jnp.bfloat16)
+        one, zero = jnp.ones((16, pw), jnp.bfloat16), jnp.zeros((16, pw), jnp.bfloat16)
+        return [jnp.where(row_id + 16.0 * k == wide_row, one, zero) for k in range(count)]
+
+    def build_source(src):
+        plane, y_num, z_num = numbers(krecv[src])
+        key = plane * grid_len + z_num
+        fold = whole((key + 0.5) * (1.0 / WIDE))
+        group_ref[src] = fold
+        for k, piece in enumerate(marks(key - fold * WIDE, WIDE // 16)):
+            hot_ref[src, 16 * k:16 * (k + 1), :] = piece
+        wide_fold = jnp.broadcast_to(fold, (16, pw)).astype(jnp.bfloat16)
+        one, zero = jnp.ones((16, pw), jnp.bfloat16), jnp.zeros((16, pw), jnp.bfloat16)
+        for k in range(folds):
+            mask_ref[src, k] = jnp.where(wide_fold == float(k), one, zero)
+        y_hot = marks(y_num, grid_len // 16)
+        table = bdot(wave_ref[me], jnp.concatenate(y_hot + y_hot, axis=0))
+        ta_ref[src] = table[:slab]
+        tb_ref[src] = table[slab:]
 
     def build_potential():
         for part in range(chunks):
             for b in range(TRIPLE):
                 for a in range(4):
                     at = (b * 4 + a) * grid_len
-                    block = potential_ref[:, TRIPLE * a + b, part * QUAD:(part + 1) * QUAD, :] * (1.0 / grid_len**3)
-                    pot_ref[part, :, :QUAD, at:at + grid_len] = block
-                    pot_ref[part, :, QUAD:, at:at + grid_len] = block
+                    for dev in range(group):
+                        row = dev * lanes // grid_len + TRIPLE * a + b
+                        block = potential_ref[part * QUAD:(part + 1) * QUAD, row, :] * (1.0 / grid_len**3)
+                        pot_ref[part, dev, :QUAD, at:at + grid_len] = block
+                        pot_ref[part, dev, QUAD:, at:at + grid_len] = block
 
     def build_coupling():
         atoms, chans = strength_ref.shape[0] // strength_ref.shape[1], strength_ref.shape[1]
@@ -457,9 +509,29 @@
         block = tiled * same
         block = 0.5 * (block + jnp.transpose(block))
         half = lax.dot_general(hot, block, (((0,), (0,)), ((), ())), precision=top_precision, preferred_element_type=jnp.float32)
-        return jnp.dot(half, hot, precision=top_precision, preferred_element_type=jnp.float32)
-
-    pl.semaphore_wait(barrier, group + bands - 2)
+        couple_ref[...] = jnp.dot(half, hot, precision=top_precision, preferred_element_type=jnp.float32)
+
+    build_coupling()
+    for load in loads:
+        load.wait()
+    build_potential()
+    spread_wait(*keys)
+
+    def build_step(src, carry):
+        build_source(src)
+        return carry
+
+    lax.fori_loop(0, group, build_step, 0)
+
+    def stack_rows(pieces):
+        return jnp.concatenate(pieces, axis=0)
+
+    cells = stack_rows([krecv[s] for s in range(group)])
+    owner = lax.broadcasted_iota(jnp.int32, (group, pw), 0).astype(jnp.float32)
+    kin_ref[...] = kinetic(*numbers(cells), owner)
+    spread_wait(*firsts)
+    for part in range(2):
+        in_vec[0, part] = stack_rows([xrecv[s, part:part + 1] for s in range(group)])
 
     sign = jnp.where(lax.broadcasted_iota(jnp.int32, (1, 2 * QUAD, 1), 1) < QUAD, -1.0, 1.0).astype(jnp.float32)
 
@@ -497,118 +569,140 @@
         high, low = two_parts(values.reshape(rows, lanes))
         return bdot(across_ref[which], jnp.concatenate([high, low, high], axis=0))
 
-    def all_sum(local, send, recv, send_sem, recv_sem, shape_at):
-        send[shape_at] = local
-        recv[shape_at, me] = local
-        for off in range(1, group):
-            pltpu.make_async_remote_copy(
-                src_ref=send.at[shape_at], dst_ref=recv.at[shape_at, me],
-                send_sem=send_sem.at[shape_at, off - 1], recv_sem=recv_sem.at[shape_at, off - 1],
-                device_id={"ga": lax.rem(me + off, group)}, device_id_type=MESH).start()
-
-    def all_sum_end(send, recv, send_sem, recv_sem, shape_at):
-        for off in range(1, group):
-            pltpu.make_async_remote_copy(
-                src_ref=send.at[shape_at], dst_ref=recv.at[shape_at, lax.rem(me + group - off, group)],
-                send_sem=send_sem.at[shape_at, off - 1], recv_sem=recv_sem.at[shape_at, off - 1],
-                device_id={"ga": lax.rem(me + off, group)}, device_id_type=MESH).wait()
-        running = recv[shape_at, 0]
-        for dev in range(1, group):
-            running = running + recv[shape_at, dev]
-        return running
-
-    def piece(turn, part, off, send, recv, send_sem, recv_sem, incoming):
-        peer = lax.rem(me + off, group)
+    def own_row(ref, turn, part):
+        return ref[turn, part, pl.ds(me, 1), :]
+
+    def put(turn):
+        for src in range(group):
+            v_re, v_im = in_vec[turn, 0, src:src + 1, :], in_vec[turn, 1, src:src + 1, :]
+            both = split_rows(ta_ref[src] * v_re + tb_ref[src] * v_im)
+            pieces = []
+            for k in range(folds):
+                for at in range(0, 2 * slab, 16):
+                    pieces.append(both[at:at + 16] * mask_ref[src, k])
+            out = bdot_t(jnp.concatenate(pieces, axis=0), hot_ref[src])
+            for k in range(folds):
+                width = min(WIDE, lanes - k * WIDE)
+                base = k * 2 * slab
+                for part in range(chunks):
+                    at = base + part * 2 * QUAD
+                    block = out[at:at + 2 * QUAD] + out[at + slab:at + slab + 2 * QUAD]
+                    field_ref[part, src, :, k * WIDE:k * WIDE + width] = block[:, :width]
+
+    def middle(part, carry):
+        triple = turn_lane(three(lane_split(field_ref[part]), 1.0), 1.0)
+        values = turn_dev(jnp.concatenate(mix_fourz(triple, 1.0), axis=-1), 1.0)
+        values = mix_devices(values, 0) * pot_ref[part].reshape(rows, lanes)
+        values = mix_devices(values, 1).reshape(group, 2 * QUAD, lanes)
+        triple = mix_fourz(lane_split(turn_dev(values, -1.0)), -1.0)
+        triple = three(turn_lane(triple, -1.0), -1.0)
+        back_ref[part] = jnp.concatenate(triple, axis=-1)
+        return carry
+
+    def partial_copy(turn, mask):
+        return pltpu.make_async_remote_copy(
+            src_ref=rsend.at[turn, mask], dst_ref=rrecv.at[turn, mask],
+            send_sem=rs_sem.at[turn, mask - 1], recv_sem=rr_sem.at[turn, mask - 1],
+            device_id={"ga": peer_of(mask)}, device_id_type=MESH)
+
+    def take(turn, mask):
+        dest = peer_of(mask)
+        both = split_rows(jnp.concatenate([back_ref[part, dest] for part in range(chunks)], axis=0))
+        if folds * WIDE > lanes:
+            both = jnp.concatenate([both, jnp.zeros((2 * slab, folds * WIDE - lanes), jnp.bfloat16)], axis=1)
+        stacked = jnp.concatenate([both[:, k * WIDE:(k + 1) * WIDE] for k in range(folds)], axis=0)
+        for at in range(0, pw, WIDE):
+            span = slice(at, at + WIDE)
+            out = bdot(stacked, hot_ref[dest, :, span])
+            fold = group_ref[dest, :, span]
+            chosen = out[:2 * slab]
+            for k in range(1, folds):
+                chosen = jnp.where(fold == float(k), out[k * 2 * slab:(k + 1) * 2 * slab], chosen)
+            value = chosen[:slab] + chosen[slab:]
+            for part, table in enumerate((ta_ref, tb_ref)):
+                rsend[turn, mask, part:part + 1, span] = jnp.sum(table[dest, :, span] * value, axis=0, keepdims=True)
+        if mask:
+            partial_copy(turn, mask).start()
+
+    def sum_copy(off, send, recv, send_sem, recv_sem, incoming):
         source = lax.rem(me + group - off, group) if incoming else me
         return pltpu.make_async_remote_copy(
-            src_ref=send.at[turn, part, peer], dst_ref=recv.at[turn, part, source],
-            send_sem=send_sem.at[turn, part, off - 1], recv_sem=recv_sem.at[turn, part, off - 1],
-            device_id={"ga": peer}, device_id_type=MESH)
-
-    def apply_h(turn, vector):
-        v_re, v_im = vector[0:1], vector[1:2]
-        fwd = (fsend, frecv, fs_sem, fr_sem)
-        back = (bsend, brecv, bs_sem, br_sem)
-
-        def put(part, carry):
-            high, low = two_parts(ta_ref[part] * v_re + tb_ref[part] * v_im)
-            out = bdot(jnp.concatenate([high, low], axis=0), hot_ref[...])
-            out = (out[:rows] + out[rows:]).reshape(group, 2 * QUAD, lanes)
-            fsend[turn, part] = out
-            frecv[turn, part, me] = fsend[turn, part, me]
-            for off in range(1, group):
-                piece(turn, part, off, *fwd, False).start()
-            return carry
-
-        lax.fori_loop(0, chunks, put, 0)
-        if turn == 0:
-            for load in loads:
-                load.wait()
-        sums = lax.dot_general(vector, proj_ref[...], (((1,), (1,)), ((), ())), precision=top_precision, preferred_element_type=jnp.float32)
-        all_sum(sums, psend, precv, ps_sem, pr_sem, turn)
-        if turn == 0:
-            build_potential()
-            shared.append(build_coupling())
-            build_turn()
-
-        def middle(part, carry):
-            for off in range(1, group):
-                piece(turn, part, off, *fwd, True).wait()
-            triple = turn_lane(three(lane_split(frecv[turn, part]), 1.0), 1.0)
-            values = turn_dev(jnp.concatenate(mix_fourz(triple, 1.0), axis=-1), 1.0)
-            values = mix_devices(values, 0) * pot_ref[part].reshape(rows, lanes)
-            values = mix_devices(values, 1).reshape(group, 2 * QUAD, lanes)
-            triple = mix_fourz(lane_split(turn_dev(values, -1.0)), -1.0)
-            triple = three(turn_lane(triple, -1.0), -1.0)
-            bsend[turn, part] = jnp.concatenate(triple, axis=-1)
-            brecv[turn, part, me] = bsend[turn, part, me]
-            for off in range(1, group):
-                piece(turn, part, off, *back, False).start()
-            return carry
-
-        lax.fori_loop(0, chunks, middle, 0)
-        sums = all_sum_end(psend, precv, ps_sem, pr_sem, turn) * (1.0 / total_pw)
+            src_ref=send, dst_ref=recv.at[source],
+            send_sem=send_sem.at[off - 1], recv_sem=recv_sem.at[off - 1],
+            device_id={"ga": lax.rem(me + off, group)}, device_id_type=MESH)
+
+    def all_sum(local, send, recv, send_sem, recv_sem):
+        send[...] = local
+        recv[me] = local
+        for off in range(1, group):
+            sum_copy(off, send, recv, send_sem, recv_sem, False).start()
+
+    def all_sum_end(send, recv, send_sem, recv_sem):
+        for off in range(1, group):
+            sum_copy(off, send, recv, send_sem, recv_sem, True).wait()
+        running = recv[0]
+        for dev in range(1, group):
+            running = running + recv[dev]
+        return running
+
+    def project(turn):
+        found = []
+        for part in range(2):
+            row = own_row(in_vec, turn, part)
+            running = proj_ref[:, :128] * row[:, :128]
+            for at in range(128, pw, 128):
+                running = running + proj_ref[:, at:at + 128] * row[:, at:at + 128]
+            found.append(jnp.sum(jnp.transpose(running), axis=0, keepdims=True))
+        return jnp.concatenate(found, axis=0)
+
+    def nonlocal_rows(sums):
         half = sums.shape[1] // 2
         pair = jnp.concatenate([
             sums[0:1, :half] + sums[1:2, half:], sums[1:2, :half] - sums[0:1, half:]], axis=0)
-        mixed = jnp.dot(pair, shared[0], precision=top_precision, preferred_element_type=jnp.float32)
+        mixed = jnp.dot(pair, couple_ref[...], precision=top_precision, preferred_element_type=jnp.float32)
         m_re, m_im = mixed[0:1], mixed[1:2]
-        weights = jnp.concatenate([
-            jnp.concatenate([m_re, -m_im], axis=1), jnp.concatenate([m_im, m_re], axis=1)], axis=0)
-        nonlocal_part = jnp.dot(weights, proj_ref[...], precision=top_precision, preferred_element_type=jnp.float32)
-        start = kin * vector + nonlocal_part
-
-        def take(part, carry):
-            run_re, run_im = carry
-            for off in range(1, group):
-                piece(turn, part, off, *back, True).wait()
-            high, low = two_parts(brecv[turn, part].reshape(rows, lanes))
-            out = bdot(jnp.concatenate([high, low], axis=0), hot_t_ref[...])
-            out = out[:rows] + out[rows:]
-            run_re = run_re + jnp.sum(ta_ref[part] * out, axis=0, keepdims=True)
-            run_im = run_im + jnp.sum(tb_ref[part] * out, axis=0, keepdims=True)
-            return run_re, run_im
-
-        run_re, run_im = lax.fori_loop(0, chunks, take, (start[0:1], start[1:2]))
-        return jnp.concatenate([run_re, run_im], axis=0)
-
-    def as_row(values):
-        total = jnp.sum(jnp.sum(values, axis=0, keepdims=True), axis=1, keepdims=True)
-        return jnp.broadcast_to(total, (1, 128))
-
-    row_count = gsend.shape[1]
-
-    def gram_sums(turn, basis, pair_list):
-        found_rows = []
+        found = []
+        for row in (jnp.concatenate([m_re, -m_im], axis=1), jnp.concatenate([m_im, m_re], axis=1)):
+            column = jnp.transpose(jnp.broadcast_to(row, (2 * half, 128)))
+            found.append(jnp.concatenate([
+                jnp.sum(proj_ref[:, at:at + 128] * column, axis=0, keepdims=True) for at in range(0, pw, 128)], axis=1))
+        return jnp.concatenate(found, axis=0)
+
+    def apply_h(turn):
+        sums = (psend.at[turn], precv.at[turn], ps_sem.at[turn], pr_sem.at[turn])
+        all_sum(project(turn), *sums)
+        put(turn)
+        lax.fori_loop(0, chunks, middle, 0)
+        start = nonlocal_rows(all_sum_end(*sums) * (1.0 / total_pw))
+        own_kin = kin_ref[pl.ds(me, 1), :]
+        start = start + own_kin * jnp.concatenate([own_row(in_vec, turn, 0), own_row(in_vec, turn, 1)], axis=0)
+        for mask in (6, 7, 4, 5, 2, 3, 1, 0):
+            take(turn, mask)
+        running = start + rsend[turn, 0]
+        for mask in range(1, group):
+            partial_copy(turn, mask).wait()
+            running = running + rrecv[turn, mask]
+        hsend[turn] = running
+        return running
+
+    def share_h(turn):
+        out = (hsend.at[turn], hrecv.at[turn], hs_sem.at[turn], hr_sem.at[turn])
+        spread_start(*out)
+        hrecv[turn, me] = hsend[turn]
+        spread_wait(*out)
+        for part in range(2):
+            out_vec[turn, part] = stack_rows([hrecv[turn, s, part:part + 1] for s in range(group)])
+
+    def vector(index):
+        ref = out_vec if index % 2 else in_vec
+        return ref[index // 2]
+
+    def gram_sums(pair_list):
+        found = {}
         for one, two, use_kin in pair_list:
-            product = basis[one] * basis[two]
-            found_rows.append(as_row(product * kin if use_kin else product))
-        found_rows += [jnp.zeros((1, 128), jnp.float32)] * (row_count - len(found_rows))
-        all_sum(jnp.concatenate(found_rows, axis=0), gsend, grecv, gs_sem, gr_sem, turn)
-        summed = all_sum_end(gsend, grecv, gs_sem, gr_sem, turn) * (1.0 / total_pw)
-        found = {}
-        for slot, (one, two, use_kin) in enumerate(pair_list):
-            value = summed[slot:slot + 1]
+            left, right = vector(one), vector(two)
+            product = left[0] * right[0] + left[1] * right[1]
+            value = total_of(product * kin_ref[...] if use_kin else product) * (1.0 / total_pw)
             found[use_kin, one, two] = value
             found[use_kin, two, one] = value
         return found
@@ -616,47 +710,48 @@
     def realize(coef_map, basis):
         running = 0.0
         for index, coef in coef_map.items():
-            running = running + (basis[index] if isinstance(coef, float) and coef == 1.0 else spread_row(coef) * basis[index])
+            running = running + (basis(index) if isinstance(coef, float) and coef == 1.0 else coef * basis(index))
         return running
 
-    def spread_row(coef):
-        return coef if isinstance(coef, float) else coef[:, 0:1]
-
     def smooth(residual, level):
-        ratio = kin / (1.5 * level[:, 0:1] + 1.0)
+        kin = kin_ref[...]
+        ratio = kin / (1.5 * level + 1.0)
         poly = 27.0 + ratio * (18.0 + ratio * (12.0 + 8.0 * ratio))
         square = ratio * ratio
         return residual * (poly / (poly + 16.0 * square * square))
 
-    shared = []
-    coeffs = coeffs_ref[:, 0, :]
-    h_zero = apply_h(0, coeffs)
-    basis = [coeffs, h_zero]
-    gram = gram_sums(0, basis, new_pairs(0, 2, (False, True)))
-    psi = {0: 1.0}
-    ham = {1: 1.0}
-    eps_zero = gram_form(gram, psi, ham, False) / (gram_form(gram, psi, psi, False) + small_eps)
-    r_map = combine([(1.0, ham), (-eps_zero, psi)])
-    level = gram_form(gram, r_map, r_map, True) / (gram_form(gram, r_map, r_map, False) + small_eps)
-    p_zero = smooth(realize(r_map, basis), level)
-    g_zero = apply_h(1, p_zero)
-    basis += [p_zero, g_zero]
-    gram.update(gram_sums(1, basis, new_pairs(2, 4, (False, True))))
-    q_map = combine([(1.0, {3: 1.0}), (-eps_zero, {2: 1.0})])
-    lam_zero = -gram_form(gram, r_map, q_map, False) / (gram_form(gram, q_map, q_map, False) + small_eps)
-    psi_one = combine([(1.0, psi), (lam_zero, {2: 1.0})])
-    h_one = combine([(1.0, ham), (lam_zero, {3: 1.0})])
-    eps_one = gram_form(gram, psi_one, h_one, False) / (gram_form(gram, psi_one, psi_one, False) + small_eps)
-    r_one = combine([(1.0, h_one), (-eps_one, psi_one)])
-    change = combine([(1.0, r_map), (-1.0, r_one)])
-    weight = gram_form(gram, r_map, change, False) / (gram_form(gram, change, change, False) + small_eps)
-    step = weight * lam_zero
-    psi_mid = combine([(1.0, psi), (step, {2: 1.0})])
-    h_mid = combine([(1.0, ham), (step, {3: 1.0})])
-    r_mid = combine([(1.0, r_map), (-weight, change)])
-    eps_mid = gram_form(gram, psi_mid, h_mid, False) / (gram_form(gram, psi_mid, psi_mid, False) + small_eps)
-    level = gram_form(gram, r_mid, r_mid, True) / (gram_form(gram, r_mid, r_mid, False) + small_eps)
-    p_one = smooth(realize(r_mid, basis), level)
+    def save(names, slot):
+        for k, value in enumerate(names):
+            save_ref[slot + k:slot + k + 1, :] = jnp.broadcast_to(value, (1, 128))
+
+    def load_saved(slot):
+        return save_ref[slot:slot + 1, 0:1]
+
+    def first_step(gram):
+        psi, ham = {0: 1.0}, {1: 1.0}
+        eps_zero = gram_form(gram, psi, ham, False) / (gram_form(gram, psi, psi, False) + small_eps)
+        return psi, ham, eps_zero, combine([(1.0, ham), (-eps_zero, psi)])
+
+    def second_step(gram):
+        psi, ham, eps_zero, r_map = first_step(gram)
+        q_map = combine([(1.0, {3: 1.0}), (-eps_zero, {2: 1.0})])
+        lam_zero = -gram_form(gram, r_map, q_map, False) / (gram_form(gram, q_map, q_map, False) + small_eps)
+        psi_one = combine([(1.0, psi), (lam_zero, {2: 1.0})])
+        h_one = combine([(1.0, ham), (lam_zero, {3: 1.0})])
+        eps_one = gram_form(gram, psi_one, h_one, False) / (gram_form(gram, psi_one, psi_one, False) + small_eps)
+        r_one = combine([(1.0, h_one), (-eps_one, psi_one)])
+        change = combine([(1.0, r_map), (-1.0, r_one)])
+        weight = gram_form(gram, r_map, change, False) / (gram_form(gram, change, change, False) + small_eps)
+        step = weight * lam_zero
+        psi_mid = combine([(1.0, psi), (step, {2: 1.0})])
+        h_mid = combine([(1.0, ham), (step, {3: 1.0})])
+        r_mid = combine([(1.0, r_map), (-weight, change)])
+        eps_mid = gram_form(gram, psi_mid, h_mid, False) / (gram_form(gram, psi_mid, psi_mid, False) + small_eps)
+        return psi_mid, h_mid, r_mid, eps_mid, step
+
+    first_pairs = new_pairs(0, 2, (False, True))
+    second_pairs = new_pairs(2, 4, (False, True))
+    gram_pairs = first_pairs + second_pairs
 
     def swap(which, send, recv, off, incoming):
         source = lax.rem(band + bands - off, bands) if incoming else band
@@ -671,57 +766,116 @@
         for off in range(1, bands):
             swap(which, send, recv, off, False).start()
 
-    share(0, nsend, nrecv, jnp.stack([realize(psi_mid, basis), p_one, realize(h_mid, basis)]))
-    g_one = apply_h(2, p_one)
-    share(1, isend, irecv, g_one)
-    basis += [p_one, g_one]
-    gram.update(gram_sums(2, basis, new_pairs(4, 6, (False,))))
+    def share_end(which, send, recv):
+        for off in range(1, bands):
+            swap(which, send, recv, off, True).wait()
+
+    def own(index):
+        ref = out_vec if index % 2 else in_vec
+        return jnp.concatenate([own_row(ref, index // 2, 0), own_row(ref, index // 2, 1)], axis=0)
+
+    def turn_step(turn, carry):
+        apply_h(turn)
+
+        @pl.when(turn == 0)
+        def _():
+            share_h(0)
+            gram = gram_sums(first_pairs)
+            save([gram[kind, one, two] for one, two, kind in first_pairs], 0)
+            r_map = first_step(gram)[3]
+            level = gram_form(gram, r_map, r_map, True) / (gram_form(gram, r_map, r_map, False) + small_eps)
+            p_zero = smooth(realize(r_map, vector), level)
+            in_vec[1] = p_zero
+
+        @pl.when(turn == 1)
+        def _():
+            share_h(1)
+            gram = gram_sums(second_pairs)
+            save([gram[kind, one, two] for one, two, kind in second_pairs], len(first_pairs))
+            for k, (one, two, kind) in enumerate(first_pairs):
+                gram[kind, one, two] = gram[kind, two, one] = load_saved(k)
+            psi_mid, h_mid, r_mid, eps_mid, step = second_step(gram)
+            level = gram_form(gram, r_mid, r_mid, True) / (gram_form(gram, r_mid, r_mid, False) + small_eps)
+            p_one = smooth(realize(r_mid, vector), level)
+            in_vec[2] = p_one
+            share(0, nsend, nrecv, jnp.stack([realize(psi_mid, own), own(4), realize(h_mid, own)]))
+
+        return carry
+
+    lax.fori_loop(0, 3, turn_step, 0)
+
+    g_own = hsend[2]
+    share(1, isend, irecv, g_own)
+    last_pairs = new_pairs(4, 6, (False,))
+
+    def own_last(index):
+        return g_own if index == 5 else own(index)
+
+    lane_id = lax.broadcasted_iota(jnp.int32, (1, 128), 1)
+    local = jnp.zeros((1, 128), jnp.float32)
+    held = [own_last(index) for index in range(6)]
+    for k, (one, two, kind) in enumerate(last_pairs):
+        local = jnp.where(lane_id == k, total_of(held[one] * held[two]), local)
+    sums = (gsend, grecv, gs_sem, gr_sem)
+    all_sum(local, *sums)
+    gram = {}
+    for k, (one, two, kind) in enumerate(gram_pairs):
+        gram[kind, one, two] = gram[kind, two, one] = load_saved(k)
+    psi_mid, h_mid, r_mid, eps_mid, step = second_step(gram)
+    summed = all_sum_end(*sums) * (1.0 / total_pw)
+    for k, (one, two, kind) in enumerate(last_pairs):
+        gram[kind, one, two] = gram[kind, two, one] = summed[:, k:k + 1]
     q_one = combine([(1.0, {5: 1.0}), (-eps_mid, {4: 1.0})])
     lam_one = -gram_form(gram, r_mid, q_one, False) / (gram_form(gram, q_one, q_one, False) + small_eps)
+    share(2, lsend, lrecv, jnp.broadcast_to(lam_one, (1, 128)))
+    share_end(0, nsend, nrecv)
+    share_end(1, isend, irecv)
+
+    pairs = [
+        [stack_rows([nrecv[o, 0, part:part + 1] for o in range(bands)] + [nrecv[o, 1, part:part + 1] for o in range(bands)]) for part in range(2)],
+        [stack_rows([nrecv[o, 2, part:part + 1] for o in range(bands)] + [irecv[o, part:part + 1] for o in range(bands)]) for part in range(2)],
+    ]
+    column_id = lax.broadcasted_iota(jnp.int32, (2 * bands, 128), 1)
+    local = jnp.zeros((2 * bands, 128), jnp.float32)
+    slot = 0
+    for o_re, o_im in pairs:
+        for mine in (0, 1):
+            m_re, m_im = nsend[mine, 0:1], nsend[mine, 1:2]
+            for product in (m_re * o_re + m_im * o_im, m_re * o_im - m_im * o_re):
+                local = jnp.where(column_id == slot, jnp.sum(product, axis=1, keepdims=True), local)
+                slot += 1
+    crossed = (csend, crecv, cs_sem, cr_sem)
+    all_sum(local, *crossed)
+
     new_map = combine([(1.0, psi_mid), (lam_one, {4: 1.0})])
     ham_new = combine([(1.0, h_mid), (lam_one, {5: 1.0})])
     norm_new = gram_form(gram, new_map, new_map, False) + small_eps
     energy = gram_form(gram, new_map, ham_new, False) / norm_new
     resid = combine([(1.0, ham_new), (-energy, new_map)])
     resid_norm = gram_form(gram, resid, resid, False) / norm_new
-    new = realize(new_map, basis)
-    new_h = realize(ham_new, basis)
-    new_ref[...] = new
-    share(2, lsend, lrecv, jnp.broadcast_to(lam_one, (8, 128)))
-    for which, send, recv in ((0, nsend, nrecv), (1, isend, irecv), (2, lsend, lrecv)):
-        for off in range(1, bands):
-            swap(which, send, recv, off, True).wait()
-    found_rows = []
-    others = []
-    for other in range(bands):
-        lam = lrecv[other, 0:1, 0:1]
-        others.append((nrecv[other, 0] + lam * nrecv[other, 1], nrecv[other, 2] + lam * irecv[other]))
-    for first in (0, 1):
-        for imag in (False, True):
-            for other in range(bands):
-                o_re = others[other][first][0:1]
-                o_im = others[other][first][1:2]
-                if imag:
-                    found_rows.append(as_row(new[0:1] * o_im - new[1:2] * o_re))
-                else:
-                    found_rows.append(as_row(new[0:1] * o_re + new[1:2] * o_im))
-    all_sum(jnp.concatenate(found_rows, axis=0), csend, crecv, cs_sem, cr_sem, 0)
-    summed = all_sum_end(csend, crecv, cs_sem, cr_sem, 0) * (1.0 / total_pw)
-    scal_ref[...] = jnp.concatenate([summed, energy, resid_norm, jnp.zeros((6, 128), jnp.float32)], axis=0)
+    new_ref[...] = nsend[0] + lam_one * nsend[1]
+    share_end(2, lsend, lrecv)
+    summed = all_sum_end(*crossed) * (1.0 / total_pw)
+    lam_rows = stack_rows([lrecv[o] for o in range(bands)])
+    mixed = summed[:bands] + lam_rows * summed[bands:]
+    result = mixed + lam_one * pltpu.roll(mixed, 126, 1)
+    scal_ref[...] = jnp.concatenate([
+        result, jnp.broadcast_to(energy, (1, 128)), jnp.broadcast_to(resid_norm, (1, 128)),
+        jnp.zeros((scal_ref.shape[0] - bands - 2, 128), jnp.float32)], axis=0)
 
 
 def finish_kernel(bands, new_ref, scal_ref, bands_ref, energy_ref, norm_ref, corr_ref, sub_ref):
     bands_ref[:, 0, :] = new_ref[...]
     lane = lax.broadcasted_iota(jnp.int32, (1, bands), 1)
-    for ref, base in ((corr_ref, 0), (sub_ref, 2 * bands)):
+    for ref, base in ((corr_ref, 0), (sub_ref, 4)):
         for part in range(2):
             row = jnp.zeros((1, bands), jnp.float32)
             for other in range(bands):
-                at = base + part * bands + other
-                row = jnp.where(lane == other, scal_ref[at:at + 1, :bands], row)
+                at = base + part
+                row = jnp.where(lane == other, scal_ref[other:other + 1, at:at + 1], row)
             ref[part] = row
-    energy_ref[0] = scal_ref[4 * bands, 0]
-    norm_ref[0] = scal_ref[4 * bands + 1, 0]
+    energy_ref[0] = scal_ref[bands, 0]
+    norm_ref[0] = scal_ref[bands + 1, 0]
 
 
 def kernel_body(coeffs, cell_map, potential, projectors, strengths, proj_atom, proj_chan):
@@ -733,63 +887,64 @@
     pw = coeffs.shape[2]
     total_pw = pw * group
     rows = group * 2 * QUAD
+    slab = chunks * 2 * QUAD
     lanes = planes * grid_len
+    folds = -(-lanes // WIDE)
     proj_rows = 2 * projectors.shape[1]
     tables = [jnp.asarray(t) for t in const_tables(grid_len, group)]
-    gram_rows = 16
-    piece_shape = (3, chunks, group, 2 * QUAD, lanes)
     dma = pltpu.SemaphoreType.DMA
     vmem = pl.BlockSpec(memory_space=pltpu.VMEM)
     far = pl.BlockSpec(memory_space=pl.ANY)
-    f32 = jnp.float32
+    f32, b16 = jnp.float32, jnp.bfloat16
+    scal_rows = 8 * (-(-(bands + 2) // 8))
+    peers = group - 1
     new, scal = pl.pallas_call(
         functools.partial(sweep_kernel, (group, bands, chunks, grid_len, total_pw, pw)),
         out_shape=(
             jax.ShapeDtypeStruct((2, pw), f32),
-            jax.ShapeDtypeStruct((4 * bands + 8, 128), f32),
+            jax.ShapeDtypeStruct((scal_rows, 128), f32),
         ),
         in_specs=[vmem, vmem, far, far] + [vmem] * 4 + [far] + [vmem] * 3,
         out_specs=(vmem, vmem),
         scratch_shapes=[
-            pltpu.VMEM((pw, lanes), jnp.bfloat16),
-            pltpu.VMEM((lanes, pw), jnp.bfloat16),
-            pltpu.VMEM((chunks, rows, pw), f32),
-            pltpu.VMEM((chunks, rows, pw), f32),
-            pltpu.VMEM((1, pw), f32),
+            pltpu.VMEM((group, WIDE, pw), b16),
+            pltpu.VMEM((group, folds, 16, pw), b16),
+            pltpu.VMEM((group, 1, pw), f32),
+            pltpu.VMEM((group, slab, pw), f32),
+            pltpu.VMEM((group, slab, pw), f32),
+            pltpu.VMEM((group, pw), f32),
             pltpu.VMEM((chunks, group, 2 * QUAD, lanes), f32),
-            pltpu.VMEM((group, planes, planes, grid_len), f32),
+            pltpu.VMEM((chunks, group, 2 * QUAD, lanes), f32),
+            pltpu.VMEM((chunks, group, 2 * QUAD, lanes), f32),
+            pltpu.VMEM((planes, grid_len, grid_len), f32),
             pltpu.VMEM((proj_rows, pw), f32),
-            pltpu.VMEM(tables[1].shape, jnp.bfloat16),
-            pltpu.SemaphoreType.DMA((3,)),
-            pltpu.VMEM(piece_shape, f32),
-            pltpu.VMEM(piece_shape, f32),
-            pltpu.VMEM(piece_shape, f32),
-            pltpu.VMEM(piece_shape, f32),
-            pltpu.VMEM((3, 2, proj_rows), f32),
-            pltpu.VMEM((3, group, 2, proj_rows), f32),
-            pltpu.VMEM((3, gram_rows, 128), f32),
-            pltpu.VMEM((3, group, gram_rows, 128), f32),
-            pltpu.VMEM((3, 2, pw), f32),
-            pltpu.VMEM((bands, 3, 2, pw), f32),
-            pltpu.VMEM((2, pw), f32),
-            pltpu.VMEM((bands, 2, pw), f32),
-            pltpu.VMEM((8, 128), f32),
-            pltpu.VMEM((bands, 8, 128), f32),
-            pltpu.VMEM((1, 4 * bands, 128), f32),
-            pltpu.VMEM((1, group, 4 * bands, 128), f32),
-            dma((3, chunks, group - 1)), dma((3, chunks, group - 1)),
-            dma((3, chunks, group - 1)), dma((3, chunks, group - 1)),
-            dma((3, group - 1)), dma((3, group - 1)),
-            dma((3, group - 1)), dma((3, group - 1)),
-            dma((3, bands - 1)), dma((3, bands - 1)),
-            dma((1, group - 1)), dma((1, group - 1)),
+            pltpu.VMEM(tables[1].shape, b16),
+            pltpu.VMEM((proj_rows // 2, proj_rows // 2), f32),
+            pltpu.VMEM((3, 2, group, pw), f32),
+            pltpu.VMEM((2, 2, group, pw), f32),
+            pltpu.VMEM((24, 128), f32),
+            dma((3,)),
+            pltpu.VMEM((1, pw), f32), pltpu.VMEM((group, 1, pw), f32),
+            pltpu.VMEM((2, pw), f32), pltpu.VMEM((group, 2, pw), f32),
+            pltpu.VMEM((3, group, 2, pw), f32), pltpu.VMEM((3, group, 2, pw), f32),
+            pltpu.VMEM((3, 2, pw), f32), pltpu.VMEM((2, group, 2, pw), f32),
+            pltpu.VMEM((3, 2, proj_rows), f32), pltpu.VMEM((3, group, 2, proj_rows), f32),
+            pltpu.VMEM((1, 128), f32), pltpu.VMEM((group, 1, 128), f32),
+            pltpu.VMEM((3, 2, pw), f32), pltpu.VMEM((bands, 3, 2, pw), f32),
+            pltpu.VMEM((2, pw), f32), pltpu.VMEM((bands, 2, pw), f32),
+            pltpu.VMEM((1, 128), f32), pltpu.VMEM((bands, 1, 128), f32),
+            pltpu.VMEM((2 * bands, 128), f32), pltpu.VMEM((group, 2 * bands, 128), f32),
+            dma((peers,)), dma((peers,)), dma((peers,)), dma((peers,)),
+            dma((3, peers)), dma((3, peers)), dma((2, peers)), dma((2, peers)),
+            dma((3, peers)), dma((3, peers)), dma((peers,)), dma((peers,)),
+            dma((3, bands - 1)), dma((3, bands - 1)), dma((peers,)), dma((peers,)),
         ],
         compiler_params=pltpu.CompilerParams(
             collective_id=0, has_side_effects=True, vmem_limit_bytes=60 * 1024 * 1024
         ),
         name="sweeps",
     )(
-        coeffs, cell_map.reshape(1, pw), potential.reshape(group, planes, planes, grid_len),
+        coeffs, cell_map.reshape(-1, 128), jnp.swapaxes(potential, 0, 1),
         projectors.reshape(proj_rows, pw), strengths.reshape(-1, strengths.shape[2]),
         proj_atom.reshape(1, -1), proj_chan.reshape(1, -1), *tables,
     )
@@ -815,8 +970,10 @@
     grid_len = potential.shape[0]
     planes = grid_len // group
     fits = (
-        planes == 4 * TRIPLE
+        group == 8
+        and planes == 4 * TRIPLE
         and 4 * grid_len % 128 == 0
+        and grid_len % 16 == 0
         and coeffs.shape[1] == 1
         and coeffs.shape[2] % 256 == 0
         and 2 * projectors.shape[1] == 128

time: 105 us -> 76.4 us (0.73)
  Pallas kernels: 100 us -> 75.5 us
  local copies, waits for them, and re-layouts: 3.61 us -> 0 us
    pallas_call x1, Pallas kernels: 98.6 us -> 74.1 us  [kernel_body(): pl.pallas_call(functools.partial(sweep_kernel, (group, bands, chunks, gri...]
    unnamed x1 -> x0, local copies, waits for them, and re-layouts: 2.3 us -> none
    reshape x1 -> x0, local copies, waits for them, and re-layouts: 1.31 us -> none  [kernel_body(): cell_map.reshape(1, pw)]
where the time goes in v1:
time: 76.4 us; the launch traced here: 76.2 us
  Pallas kernels  75.5 us (99%)
    pallas_call x1, Pallas kernels, kernel_body(): pl.pallas_call(functools.partial(sweep_kernel, (group, bands, chunks, gri...  74.1 us

profile of v1, /device:TPU:0, one launch (start us, length us, event | category | flops | bytes accessed | tf_op | source)
XLA Modules:
  0.0 76.2 jit_solution(6885454641021352601)
XLA Ops:
  0.6 74.1 %sweeps.1 = (f32[2,2304]{1,0:T(2,128)}, f32[8,128]{1,0:T(8,128)}) custom-call(f32[2,1,2304]{2,1,0:T(1,128)} %coeffs_ref.1, s32[18,128]{1,0:T(8,128)} %bitcast.9, f32[12,96,96]{2,1,0:T(8,128)} %bitcast.7, f32[128,2304]{1,0:T(8,128)} %bitcast.6, f32[64,8]{1,0:T(8,128)} %bitcast.8, s32[1,64]{1,0:T(1,128)} %bitcast.10, s32[1,64]{1,0:T(1,128)} %bitcast.11, ...), custom_call_target="tpu_custom_call" | custom-call | tf_op jit(solution)/shard_map/sweeps/pallas_call | solution.py:901
  74.8 1.4 %finish.1 = (f32[2,1,2304]{2,1,0:T(1,128)}, f32[1]{0:T(128)}, f32[1]{0:T(128)}, f32[2,1,4]{2,1,0:T(1,128)}, f32[2,1,4]{2,1,0:T(1,128)}) custom-call(f32[2,2304]{1,0:T(2,128)} %get-tuple-element.7.new_ref, f32[8,128]{1,0:T(8,128)} %get-tuple-element.8.scal_ref), custom_call_target="tpu_custom_call" | custom-call | tf_op jit(solution)/shard_map/finish/pallas_call | solution.py:953

commit v2 on v1

--- a/solution.py
+++ b/solution.py
@@ -297,8 +297,6 @@
     return (new_bands, energy, residual_norm, correlation, subspace)
 
 
-QUAD = 4
-TRIPLE = 3
 WIDE = 256
 MESH = pl.DeviceIdType.MESH
 
@@ -311,48 +309,28 @@
 
 def const_tables(grid_len, group):
     planes = grid_len // group
-    chunks = planes // QUAD
     unit = 2.0 * np.pi / grid_len
     quarter = grid_len / 4.0
-    dev = np.arange(group)[:, None, None, None]
-    chunk = np.arange(chunks)[None, :, None, None]
-    part = np.arange(2)[None, None, :, None]
-    inner = np.arange(QUAD)[None, None, None, :]
-    y_real = (dev * planes + chunk * QUAD + inner + 0 * part).reshape(group, -1)
-    part_row = (part + 0 * (dev + chunk + inner)).reshape(group, -1)
+    main = list(range(8))
+    rest = list(range(8, planes))
+    y_in = np.array(main + rest + rest + main)
+    part_row = np.array([0] * planes + [1] * planes)
+    y_real = np.arange(group)[:, None] * planes + y_in[None, :]
     freq = np.arange(grid_len)
     phase = (y_real[..., None] * freq) % grid_len
-    tab_a = np.cos(unit * (phase - quarter * part_row[..., None]))
-    tab_b = np.cos(unit * (phase + quarter * (1 - part_row[..., None])))
+    tab_a = np.cos(unit * (phase - quarter * part_row[:, None]))
+    tab_b = np.cos(unit * (phase + quarter * (1 - part_row[:, None])))
     high, low = split_const(np.concatenate([tab_a, tab_b], axis=1))
     wave = np.concatenate([high, low], axis=2)
-    four = np.repeat(np.arange(4), grid_len)
-    zed = np.tile(freq, 4)
-    theta = 2.0 * np.pi * ((four[:, None] * four[None, :] % 4) / 4.0
-                           + (zed[:, None] * zed[None, :] % grid_len) / grid_len)
-    fourz = split_const(np.concatenate([np.cos(theta), np.sin(theta)], axis=1))
-    dft = 2.0 * np.pi * np.outer(np.arange(group), np.arange(group)) / group
-    real_mix = np.zeros((group, 2, QUAD, group, 2, QUAD))
-    for row in range(QUAD):
-        real_mix[:, 0, row, :, 0, row] = np.cos(dft)
-        real_mix[:, 1, row, :, 1, row] = np.cos(dft)
-        real_mix[:, 0, row, :, 1, row] = -np.sin(dft)
-        real_mix[:, 1, row, :, 0, row] = np.sin(dft)
-    size = group * 2 * QUAD
-    real_mix = real_mix.reshape(size, size)
-
-    def stacked(mat):
-        high, low = split_const(mat)
-        return np.concatenate([high, high, low], axis=1)
-
-    across = np.stack([stacked(real_mix), stacked(real_mix.T)])
-    b_lane = np.repeat(np.arange(TRIPLE), 4 * grid_len)
-    a_lane = np.tile(np.repeat(np.arange(4), grid_len), TRIPLE)
-    one = 2.0 * np.pi * (a_lane * b_lane) / planes
-    two = unit * np.outer(np.arange(group), TRIPLE * a_lane + b_lane)
-    lane_tw = np.stack([np.cos(one), np.sin(one)]).astype(np.float32)[:, None, :]
-    dev_tw = np.stack([np.cos(two), np.sin(two)]).astype(np.float32)[:, :, None, :]
-    return wave, fourz, across, lane_tw, dev_tw
+    theta = unit * (np.outer(freq, freq) % grid_len)
+    turn = np.zeros((2, 128, 2, 128))
+    turn[0, :grid_len, 0, :grid_len] = np.cos(theta)
+    turn[0, :grid_len, 1, :grid_len] = np.sin(theta)
+    turn[1, :grid_len, 0, :grid_len] = -np.sin(theta)
+    turn[1, :grid_len, 1, :grid_len] = np.cos(theta)
+    turn = turn.reshape(256, 256)
+    zed = np.concatenate([split_const(turn), split_const(turn.T)], axis=0)
+    return wave, zed
 
 
 def two_parts(values):
@@ -378,36 +356,86 @@
     return jnp.sum(jnp.sum(values, axis=0, keepdims=True), axis=1, keepdims=True)
 
 
+def c_add(one, two):
+    return one[0] + two[0], one[1] + two[1]
+
+
+def c_sub(one, two):
+    return one[0] - two[0], one[1] - two[1]
+
+
+def c_turn(one, direction):
+    return (-one[1], one[0]) if direction > 0 else (one[1], -one[0])
+
+
+def c_mul(one, cos_val, sin_val):
+    return one[0] * cos_val - one[1] * sin_val, one[0] * sin_val + one[1] * cos_val
+
+
+def c_scale(one, factor):
+    return one[0] * factor, one[1] * factor
+
+
+def three_point(items, direction):
+    total = c_add(items[1], items[2])
+    side = c_scale(c_turn(c_sub(items[1], items[2]), direction), 0.8660254037844386)
+    base = c_sub(items[0], c_scale(total, 0.5))
+    return [c_add(items[0], total), c_add(base, side), c_sub(base, side)]
+
+
+def four_point(items, direction):
+    even, odd = c_add(items[0], items[2]), c_add(items[1], items[3])
+    low, high = c_sub(items[0], items[2]), c_turn(c_sub(items[1], items[3]), direction)
+    return [c_add(even, odd), c_add(low, high), c_sub(even, odd), c_sub(low, high)]
+
+
+def eight_point(items, direction):
+    even = four_point(items[0::2], direction)
+    odd = four_point(items[1::2], direction)
+    root = 0.7071067811865476
+    turned = [
+        odd[0],
+        c_scale(c_add(odd[1], c_turn(odd[1], direction)), root),
+        c_turn(odd[2], direction),
+        c_scale(c_sub(c_turn(odd[3], direction), odd[3]), root),
+    ]
+    return [c_add(e, o) for e, o in zip(even, turned)] + [c_sub(e, o) for e, o in zip(even, turned)]
+
+
+def twelve_point(items, direction):
+    fours = [four_point([items[(4 * a + 3 * b) % 12] for b in range(4)], direction) for a in range(3)]
+    threes = [three_point([fours[a][v] for a in range(3)], direction) for v in range(4)]
+    return [threes[v % 4][v % 3] for v in range(12)]
+
+
 def sweep_kernel(
     dims,
     coeffs_ref, cell_ref, potential_hbm, proj_hbm, strength_ref, atom_ref, chan_ref,
-    wave_ref, fourz_hbm, across_ref, lane_ref, dev_ref,
+    wave_ref, zed_ref,
     new_ref, scal_ref,
-    hot_ref, mask_ref, group_ref, ta_ref, tb_ref, kin_ref, field_ref, back_ref,
-    pot_ref, potential_ref, proj_ref, fourz_ref, couple_ref, in_vec, out_vec, save_ref, in_sem,
+    hot_ref, mask_ref, group_ref, ta_ref, tb_ref, kin_ref, work_ref, left_ref,
+    pot_ref, potential_ref, proj_ref, couple_ref, in_vec, out_vec, save_ref, in_sem,
     ksend, krecv, xsend, xrecv, rsend, rrecv, hsend, hrecv, psend, precv,
     gsend, grecv, nsend, nrecv, isend, irecv, lsend, lrecv, csend, crecv,
     ks_sem, kr_sem, xs_sem, xr_sem, rs_sem, rr_sem, hs_sem, hr_sem, ps_sem, pr_sem,
     gs_sem, gr_sem, ns_sem, nr_sem, cs_sem, cr_sem,
 ):
-    group, bands, chunks, grid_len, total_pw, pw = dims
-    rows = group * 2 * QUAD
-    slab = chunks * 2 * QUAD
-    lanes = TRIPLE * 4 * grid_len
-    quad_lanes = 4 * grid_len
-    folds = -(-lanes // WIDE)
+    group, bands, planes, grid_len, total_pw, pw = dims
+    slab = 2 * planes
+    folds = planes // 2
+    half = group // 2
     tiles = pw // 128
     me = lax.axis_index("ga")
     band = lax.axis_index("band")
     sides = [1 - 2 * lax.rem(me // (1 << bit), 2) for bit in range(3)]
 
     def peer_of(mask):
-        return me + sum((sides[bit] << bit) if mask >> bit & 1 else 0 for bit in range(3))
+        return me + sum(sides[bit] * ((mask // (1 << bit)) % 2) * (1 << bit) for bit in range(3))
 
     loads = [
         pltpu.make_async_copy(source, target, in_sem.at[k])
         for k, (source, target) in enumerate(
-            ((proj_hbm, proj_ref), (potential_hbm, potential_ref), (fourz_hbm, fourz_ref)))
+            ((proj_hbm, proj_ref), (potential_hbm, potential_ref)))
     ]
     for load in loads:
         load.start()
@@ -472,10 +500,9 @@
 
     def build_source(src):
         plane, y_num, z_num = numbers(krecv[src])
-        key = plane * grid_len + z_num
-        fold = whole((key + 0.5) * (1.0 / WIDE))
+        fold = whole((plane + 0.5) * 0.5)
         group_ref[src] = fold
-        for k, piece in enumerate(marks(key - fold * WIDE, WIDE // 16)):
+        for k, piece in enumerate(marks((plane - 2.0 * fold) * 128.0 + z_num, WIDE // 16)):
             hot_ref[src, 16 * k:16 * (k + 1), :] = piece
         wide_fold = jnp.broadcast_to(fold, (16, pw)).astype(jnp.bfloat16)
         one, zero = jnp.ones((16, pw), jnp.bfloat16), jnp.zeros((16, pw), jnp.bfloat16)
@@ -487,15 +514,20 @@
         tb_ref[src] = table[slab:]
 
     def build_potential():
-        for part in range(chunks):
-            for b in range(TRIPLE):
-                for a in range(4):
-                    at = (b * 4 + a) * grid_len
-                    for dev in range(group):
-                        row = dev * lanes // grid_len + TRIPLE * a + b
-                        block = potential_ref[part * QUAD:(part + 1) * QUAD, row, :] * (1.0 / grid_len**3)
-                        pot_ref[part, dev, :QUAD, at:at + grid_len] = block
-                        pot_ref[part, dev, QUAD:, at:at + grid_len] = block
+        pad = jnp.zeros((8, 128 - grid_len), jnp.float32)
+
+        def put_tile(v, slot, block):
+            pot_ref[v, slot] = jnp.concatenate([block * (1.0 / grid_len**3), pad], axis=1)
+
+        def lines(x_real, first, count):
+            return potential_ref[pl.ds(first * grid_len + x_real, count, stride=grid_len), :]
+
+        for v in range(planes):
+            for u in range(group):
+                put_tile(v, u, lines(v + planes * u, 0, 8))
+            for t in range(half):
+                put_tile(v, group + t, jnp.concatenate([
+                    lines(v + planes * 2 * t, 8, planes - 8), lines(v + planes * (2 * t + 1), 8, planes - 8)], axis=0))
 
     def build_coupling():
         atoms, chans = strength_ref.shape[0] // strength_ref.shape[1], strength_ref.shape[1]
@@ -511,17 +543,18 @@
         half = lax.dot_general(hot, block, (((0,), (0,)), ((), ())), precision=top_precision, preferred_element_type=jnp.float32)
         couple_ref[...] = jnp.dot(half, hot, precision=top_precision, preferred_element_type=jnp.float32)
 
+    build_source(me)
     build_coupling()
     for load in loads:
         load.wait()
     build_potential()
-    spread_wait(*keys)
-
-    def build_step(src, carry):
-        build_source(src)
+
+    def build_step(mask, carry):
+        spread_copy(mask, *keys, True).wait()
+        build_source(peer_of(mask))
         return carry
 
-    lax.fori_loop(0, group, build_step, 0)
+    lax.fori_loop(1, group, build_step, 0)
 
     def stack_rows(pieces):
         return jnp.concatenate(pieces, axis=0)
@@ -533,71 +566,101 @@
     for part in range(2):
         in_vec[0, part] = stack_rows([xrecv[s, part:part + 1] for s in range(group)])
 
-    sign = jnp.where(lax.broadcasted_iota(jnp.int32, (1, 2 * QUAD, 1), 1) < QUAD, -1.0, 1.0).astype(jnp.float32)
-
-    def times_i(values):
-        return pltpu.roll(values, QUAD, 1) * sign
-
-    def lane_split(values):
-        return [values[..., k * quad_lanes:(k + 1) * quad_lanes] for k in range(TRIPLE)]
-
-    def mix_fourz(triple, direction):
-        stacked = jnp.concatenate([t.reshape(rows, quad_lanes) for t in triple], axis=0)
+    upper = lax.broadcasted_iota(jnp.int32, (8, 128), 0) < 4
+    flip = jnp.where(upper, 1.0, -1.0).astype(jnp.float32)
+
+    def swap_half(values):
+        return pltpu.roll(values, 4, 0)
+
+    def halves(low, high):
+        return low if low == high else jnp.where(upper, low, high)
+
+    def lane_turn(s, v, paired):
+        angle = [2.0 * np.pi * ((k * v) % grid_len) / grid_len for k in (s, s + half)]
+        cos_val, sin_val = [float(np.cos(a)) for a in angle], [float(np.sin(a)) for a in angle]
+        if paired:
+            return halves(*cos_val), halves(*sin_val)
+        return cos_val[0], sin_val[0]
+
+    def twist(item, s, v, paired, direction):
+        if v == 0 or (s == 0 and not paired):
+            return item
+        cos_val, sin_val = lane_turn(s, v, paired)
+        return c_mul(item, cos_val, sin_val if direction > 0 else -sin_val)
+
+    def z_turn(tiles, which):
+        stacked = jnp.concatenate([jnp.concatenate(list(t), axis=1) for t in tiles], axis=0)
         high, low = two_parts(stacked)
-        out = bdot(high, fourz_ref[0]) + bdot(low, fourz_ref[0]) + bdot(high, fourz_ref[1])
-        out = out.reshape(TRIPLE * group, 2 * QUAD, 2 * quad_lanes)
-        mixed = out[..., :quad_lanes] + direction * times_i(out[..., quad_lanes:])
-        return [mixed[k * group:(k + 1) * group] for k in range(TRIPLE)]
-
-    def turn_lane(triple, direction):
-        done = [triple[0]]
-        for k in range(1, TRIPLE):
-            at = slice(k * quad_lanes, (k + 1) * quad_lanes)
-            done.append(triple[k] * lane_ref[0, :, at][None] + direction * times_i(triple[k]) * lane_ref[1, :, at][None])
-        return done
-
-    def three(triple, direction):
-        total = triple[1] + triple[2]
-        diff = times_i(triple[1] - triple[2]) * (direction * 0.8660254037844386)
-        base = triple[0] - 0.5 * total
-        return [triple[0] + total, base + diff, base - diff]
-
-    def turn_dev(values, direction):
-        return values * dev_ref[0] + direction * times_i(values) * dev_ref[1]
-
-    def mix_devices(values, which):
-        high, low = two_parts(values.reshape(rows, lanes))
-        return bdot(across_ref[which], jnp.concatenate([high, low, high], axis=0))
+        out = bdot(high, zed_ref[which]) + bdot(low, zed_ref[which]) + bdot(high, zed_ref[which + 1])
+        return [(out[8 * k:8 * k + 8, :128], out[8 * k:8 * k + 8, 128:]) for k in range(len(tiles))]
+
+    def keep(slot, v, item):
+        work_ref[0, v, slot] = item[0]
+        work_ref[1, v, slot] = item[1]
+
+    def kept(slot, v):
+        return work_ref[0, v, slot], work_ref[1, v, slot]
 
     def own_row(ref, turn, part):
         return ref[turn, part, pl.ds(me, 1), :]
 
-    def put(turn):
-        for src in range(group):
-            v_re, v_im = in_vec[turn, 0, src:src + 1, :], in_vec[turn, 1, src:src + 1, :]
-            both = split_rows(ta_ref[src] * v_re + tb_ref[src] * v_im)
-            pieces = []
+    def put(turn, src):
+        v_re, v_im = in_vec[turn, 0, src:src + 1, :], in_vec[turn, 1, src:src + 1, :]
+        both = split_rows(ta_ref[src] * v_re + tb_ref[src] * v_im)
+        pieces = []
+        for k in range(folds):
+            for at in range(0, 2 * slab, 16):
+                pieces.append(both[at:at + 16] * mask_ref[src, k])
+        out = bdot_t(jnp.concatenate(pieces, axis=0), hot_ref[src])
+        tiles = []
+        for k in range(folds):
+            base = k * 2 * slab
+            block = out[base:base + slab] + out[base + slab:base + 2 * slab]
+            for at in (0, 128):
+                tiles.append([block[8 * t:8 * t + 8, at:at + 128] for t in range(3)])
+        return tiles
+
+    def forward_pair(turn, s):
+        low, high = put(turn, s), put(turn, s + half)
+        rest = [(
+            jnp.where(upper, a[1], swap_half(b[1])), jnp.where(upper, swap_half(a[1]), b[1]),
+        ) for a, b in zip(low, high)]
+        turned = z_turn([(a[0], a[2]) for a in low] + [(b[0], b[2]) for b in high] + rest, 0)
+        for k, (slot, first, paired) in enumerate(((s, s, False), (s + half, s + half, False), (group + s, s, True))):
+            for v, item in enumerate(twelve_point(turned[k * planes:(k + 1) * planes], 1)):
+                keep(slot, v, twist(item, first, v, paired, 1))
+
+    def cross(item):
+        return tuple(swap_half(x) + x * flip for x in item)
+
+    def half_turn(item, s, direction):
+        if s == 0:
+            return item
+        angle = 2.0 * np.pi * s / group
+        return c_mul(item, halves(1.0, float(np.cos(angle))), direction * halves(0.0, float(np.sin(angle))))
+
+    def middle(v):
+        items = eight_point([kept(s, v) for s in range(group)], 1)
+        items = [c_scale(item, pot_ref[v, u]) for u, item in enumerate(items)]
+        for s, item in enumerate(eight_point(items, -1)):
+            keep(s, v, twist(item, s, v, False, -1))
+        items = four_point([half_turn(cross(kept(group + s, v)), s, 1) for s in range(half)], 1)
+        items = [c_scale(item, pot_ref[v, group + t]) for t, item in enumerate(items)]
+        for s, item in enumerate(four_point(items, -1)):
+            keep(group + s, v, twist(cross(half_turn(item, s, -1)), s, v, True, -1))
+
+    def backward_pair(s):
+        spread = []
+        for slot in (s, s + half, group + s):
+            spread += twelve_point([kept(slot, v) for v in range(planes)], -1)
+        turned = z_turn(spread, 2)
+        low, high, rest = [turned[k * planes:(k + 1) * planes] for k in range(3)]
+        low = [(a[0], jnp.where(upper, r[0], swap_half(r[1])), a[1]) for a, r in zip(low, rest)]
+        high = [(b[0], jnp.where(upper, swap_half(r[0]), r[1]), b[1]) for b, r in zip(high, rest)]
+        for dest, tiles in ((s, low), (s + half, high)):
             for k in range(folds):
-                for at in range(0, 2 * slab, 16):
-                    pieces.append(both[at:at + 16] * mask_ref[src, k])
-            out = bdot_t(jnp.concatenate(pieces, axis=0), hot_ref[src])
-            for k in range(folds):
-                width = min(WIDE, lanes - k * WIDE)
-                base = k * 2 * slab
-                for part in range(chunks):
-                    at = base + part * 2 * QUAD
-                    block = out[at:at + 2 * QUAD] + out[at + slab:at + slab + 2 * QUAD]
-                    field_ref[part, src, :, k * WIDE:k * WIDE + width] = block[:, :width]
-
-    def middle(part, carry):
-        triple = turn_lane(three(lane_split(field_ref[part]), 1.0), 1.0)
-        values = turn_dev(jnp.concatenate(mix_fourz(triple, 1.0), axis=-1), 1.0)
-        values = mix_devices(values, 0) * pot_ref[part].reshape(rows, lanes)
-        values = mix_devices(values, 1).reshape(group, 2 * QUAD, lanes)
-        triple = mix_fourz(lane_split(turn_dev(values, -1.0)), -1.0)
-        triple = three(turn_lane(triple, -1.0), -1.0)
-        back_ref[part] = jnp.concatenate(triple, axis=-1)
-        return carry
+                block = jnp.concatenate([jnp.concatenate(tiles[2 * k + m], axis=0) for m in range(2)], axis=1)
+                left_ref[dest, k * 2 * slab:(k + 1) * 2 * slab, :] = split_rows(block)
 
     def partial_copy(turn, mask):
         return pltpu.make_async_remote_copy(
@@ -607,10 +670,7 @@
 
     def take(turn, mask):
         dest = peer_of(mask)
-        both = split_rows(jnp.concatenate([back_ref[part, dest] for part in range(chunks)], axis=0))
-        if folds * WIDE > lanes:
-            both = jnp.concatenate([both, jnp.zeros((2 * slab, folds * WIDE - lanes), jnp.bfloat16)], axis=1)
-        stacked = jnp.concatenate([both[:, k * WIDE:(k + 1) * WIDE] for k in range(folds)], axis=0)
+        stacked = left_ref[dest]
         for at in range(0, pw, WIDE):
             span = slice(at, at + WIDE)
             out = bdot(stacked, hot_ref[dest, :, span])
@@ -671,13 +731,18 @@
     def apply_h(turn):
         sums = (psend.at[turn], precv.at[turn], ps_sem.at[turn], pr_sem.at[turn])
         all_sum(project(turn), *sums)
-        put(turn)
-        lax.fori_loop(0, chunks, middle, 0)
+        for s in range(half):
+            forward_pair(turn, s)
+        for v in range(planes):
+            middle(v)
+        for masks in ((6, 7, 2, 3), (4, 5, 1, 0)):
+            for mask in masks[:2]:
+                backward_pair(lax.rem(peer_of(mask), half))
+            for mask in masks:
+                take(turn, mask)
         start = nonlocal_rows(all_sum_end(*sums) * (1.0 / total_pw))
         own_kin = kin_ref[pl.ds(me, 1), :]
         start = start + own_kin * jnp.concatenate([own_row(in_vec, turn, 0), own_row(in_vec, turn, 1)], axis=0)
-        for mask in (6, 7, 4, 5, 2, 3, 1, 0):
-            take(turn, mask)
         running = start + rsend[turn, 0]
         for mask in range(1, group):
             partial_copy(turn, mask).wait()
@@ -883,13 +948,11 @@
     bands = lax.axis_size("band")
     grid_len = potential.shape[0]
     planes = grid_len // group
-    chunks = planes // QUAD
     pw = coeffs.shape[2]
     total_pw = pw * group
-    rows = group * 2 * QUAD
-    slab = chunks * 2 * QUAD
-    lanes = planes * grid_len
-    folds = -(-lanes // WIDE)
+    slab = 2 * planes
+    folds = planes // 2
+    tile_count = group + group // 2
     proj_rows = 2 * projectors.shape[1]
     tables = [jnp.asarray(t) for t in const_tables(grid_len, group)]
     dma = pltpu.SemaphoreType.DMA
@@ -899,12 +962,12 @@
     scal_rows = 8 * (-(-(bands + 2) // 8))
     peers = group - 1
     new, scal = pl.pallas_call(
-        functools.partial(sweep_kernel, (group, bands, chunks, grid_len, total_pw, pw)),
+        functools.partial(sweep_kernel, (group, bands, planes, grid_len, total_pw, pw)),
         out_shape=(
             jax.ShapeDtypeStruct((2, pw), f32),
             jax.ShapeDtypeStruct((scal_rows, 128), f32),
         ),
-        in_specs=[vmem, vmem, far, far] + [vmem] * 4 + [far] + [vmem] * 3,
+        in_specs=[vmem, vmem, far, far] + [vmem] * 5,
         out_specs=(vmem, vmem),
         scratch_shapes=[
             pltpu.VMEM((group, WIDE, pw), b16),
@@ -913,17 +976,16 @@
             pltpu.VMEM((group, slab, pw), f32),
             pltpu.VMEM((group, slab, pw), f32),
             pltpu.VMEM((group, pw), f32),
-            pltpu.VMEM((chunks, group, 2 * QUAD, lanes), f32),
-            pltpu.VMEM((chunks, group, 2 * QUAD, lanes), f32),
-            pltpu.VMEM((chunks, group, 2 * QUAD, lanes), f32),
-            pltpu.VMEM((planes, grid_len, grid_len), f32),
+            pltpu.VMEM((2, planes, tile_count, 8, 128), f32),
+            pltpu.VMEM((group, folds * 2 * slab, WIDE), b16),
+            pltpu.VMEM((planes, tile_count, 8, 128), f32),
+            pltpu.VMEM((planes * grid_len, grid_len), f32),
             pltpu.VMEM((proj_rows, pw), f32),
-            pltpu.VMEM(tables[1].shape, b16),
             pltpu.VMEM((proj_rows // 2, proj_rows // 2), f32),
             pltpu.VMEM((3, 2, group, pw), f32),
             pltpu.VMEM((2, 2, group, pw), f32),
             pltpu.VMEM((24, 128), f32),
-            dma((3,)),
+            dma((2,)),
             pltpu.VMEM((1, pw), f32), pltpu.VMEM((group, 1, pw), f32),
             pltpu.VMEM((2, pw), f32), pltpu.VMEM((group, 2, pw), f32),
             pltpu.VMEM((3, group, 2, pw), f32), pltpu.VMEM((3, group, 2, pw), f32),
@@ -944,7 +1006,7 @@
         ),
         name="sweeps",
     )(
-        coeffs, cell_map.reshape(-1, 128), jnp.swapaxes(potential, 0, 1),
+        coeffs, cell_map.reshape(-1, 128), jnp.swapaxes(potential, 0, 1).reshape(planes * grid_len, grid_len),
         projectors.reshape(proj_rows, pw), strengths.reshape(-1, strengths.shape[2]),
         proj_atom.reshape(1, -1), proj_chan.reshape(1, -1), *tables,
     )
@@ -971,9 +1033,7 @@
     planes = grid_len // group
     fits = (
         group == 8
-        and planes == 4 * TRIPLE
-        and 4 * grid_len % 128 == 0
-        and grid_len % 16 == 0
+        and planes == 12
         and coeffs.shape[1] == 1
         and coeffs.shape[2] % 256 == 0
         and 2 * projectors.shape[1] == 128

time: 76.4 us -> 67.9 us (0.89)
  Pallas kernels: 75.5 us -> 67.1 us
    pallas_call x1, Pallas kernels: 74.1 us -> 65.7 us  [kernel_body(): pl.pallas_call(functools.partial(sweep_kernel, (group, bands, planes, gri...]
where the time goes in v2:
time: 67.9 us; the launch traced here: 67.7 us
  Pallas kernels  67.1 us (99%)
    pallas_call x1, Pallas kernels, kernel_body(): pl.pallas_call(functools.partial(sweep_kernel, (group, bands, planes, gri...  65.7 us
    pallas_call x1, Pallas kernels, kernel_body(): pl.pallas_call(functools.partial(finish_kernel, bands), out_shape=(jax.Sh...  1.39 us

profile of v2, /device:TPU:0, one launch (start us, length us, event | category | flops | bytes accessed | tf_op | source)
XLA Modules:
  0.0 67.7 jit_solution(323915473110614354)
XLA Ops:
  0.6 65.7 %sweeps.1 = (f32[2,2304]{1,0:T(2,128)}, f32[8,128]{1,0:T(8,128)}) custom-call(f32[2,1,2304]{2,1,0:T(1,128)} %coeffs_ref.1, s32[18,128]{1,0:T(8,128)} %bitcast.11, f32[1152,96]{1,0:T(8,128)} %bitcast.9, f32[128,2304]{1,0:T(8,128)} %bitcast.8, f32[64,8]{1,0:T(8,128)} %bitcast.10, s32[1,64]{1,0:T(1,128)} %bitcast.12, s32[1,64]{1,0:T(1,128)} %bitcast.13, ...), custom_call_target="tpu_custom_call" | custom-call | tf_op jit(solution)/shard_map/sweeps/pallas_call | solution.py:964
  66.4 1.4 %finish.1 = (f32[2,1,2304]{2,1,0:T(1,128)}, f32[1]{0:T(128)}, f32[1]{0:T(128)}, f32[2,1,4]{2,1,0:T(1,128)}, f32[2,1,4]{2,1,0:T(1,128)}) custom-call(f32[2,2304]{1,0:T(2,128)} %get-tuple-element.7.new_ref, f32[8,128]{1,0:T(8,128)} %get-tuple-element.8.scal_ref), custom_call_target="tpu_custom_call" | custom-call | tf_op jit(solution)/shard_map/finish/pallas_call | solution.py:1015

commit v3 on v2

--- a/solution.py
+++ b/solution.py
@@ -410,11 +410,12 @@
 
 def sweep_kernel(
     dims,
-    coeffs_ref, cell_ref, potential_hbm, proj_hbm, strength_ref, atom_ref, chan_ref,
-    wave_ref, zed_ref,
-    new_ref, scal_ref,
+    coeffs_hbm, cell_hbm, potential_hbm, proj_hbm, strength_hbm, atom_hbm, chan_hbm,
+    wave_hbm, zed_hbm,
+    new_hbm, scal_hbm,
     hot_ref, mask_ref, group_ref, ta_ref, tb_ref, kin_ref, work_ref, left_ref,
-    pot_ref, potential_ref, proj_ref, couple_ref, in_vec, out_vec, save_ref, in_sem,
+    pot_ref, potential_ref, proj_ref, couple_ref, in_vec, out_vec, save_ref,
+    strength_ref, atom_ref, chan_ref, wave_ref, zed_ref, new_ref, scal_ref, in_sem,
     ksend, krecv, xsend, xrecv, rsend, rrecv, hsend, hrecv, psend, precv,
     gsend, grecv, nsend, nrecv, isend, irecv, lsend, lrecv, csend, crecv,
     ks_sem, kr_sem, xs_sem, xr_sem, rs_sem, rr_sem, hs_sem, hr_sem, ps_sem, pr_sem,
@@ -434,21 +435,20 @@
 
     loads = [
         pltpu.make_async_copy(source, target, in_sem.at[k])
-        for k, (source, target) in enumerate(
-            ((proj_hbm, proj_ref), (potential_hbm, potential_ref)))
+        for k, (source, target) in enumerate((
+            (cell_hbm, ksend), (coeffs_hbm, xsend), (wave_hbm.at[me], wave_ref), (strength_hbm, strength_ref),
+            (atom_hbm, atom_ref), (chan_hbm, chan_ref), (potential_hbm, potential_ref), (proj_hbm, proj_ref),
+            (zed_hbm, zed_ref)))
     ]
-    for load in loads:
-        load.start()
     barrier = pltpu.get_barrier_semaphore()
     for mask in range(1, group):
         pl.semaphore_signal(barrier, inc=1, device_id={"ga": peer_of(mask)}, device_id_type=MESH)
     for off in range(1, bands):
         pl.semaphore_signal(barrier, inc=1, device_id={"band": lax.rem(band + off, bands)}, device_id_type=MESH)
-
-    cell = cell_ref[...].astype(jnp.float32)
-    for k in range(tiles):
-        ksend[:, k * 128:(k + 1) * 128] = cell[k:k + 1]
-    xsend[...] = coeffs_ref[:, 0, :]
+    for load in loads:
+        load.start()
+    for load in loads[:2]:
+        load.wait()
 
     far_first = (6, 7, 4, 5, 2, 3, 1)
 
@@ -487,6 +487,10 @@
         y_num = whole((in_plane + 0.5) * (1.0 / grid_len))
         return plane, y_num, in_plane - y_num * grid_len
 
+    def cell_row(src):
+        cell = krecv[src].astype(jnp.float32)
+        return jnp.concatenate([cell[k:k + 1] for k in range(tiles)], axis=1)
+
     def kinetic(plane, y_num, z_num, device):
         f_x = signed(plane * group + device)
         f_y, f_z = signed(y_num), signed(z_num)
@@ -499,7 +503,7 @@
         return [jnp.where(row_id + 16.0 * k == wide_row, one, zero) for k in range(count)]
 
     def build_source(src):
-        plane, y_num, z_num = numbers(krecv[src])
+        plane, y_num, z_num = numbers(cell_row(src))
         fold = whole((plane + 0.5) * 0.5)
         group_ref[src] = fold
         for k, piece in enumerate(marks((plane - 2.0 * fold) * 128.0 + z_num, WIDE // 16)):
@@ -509,7 +513,7 @@
         for k in range(folds):
             mask_ref[src, k] = jnp.where(wide_fold == float(k), one, zero)
         y_hot = marks(y_num, grid_len // 16)
-        table = bdot(wave_ref[me], jnp.concatenate(y_hot + y_hot, axis=0))
+        table = bdot(wave_ref[...], jnp.concatenate(y_hot + y_hot, axis=0))
         ta_ref[src] = table[:slab]
         tb_ref[src] = table[slab:]
 
@@ -543,28 +547,25 @@
         half = lax.dot_general(hot, block, (((0,), (0,)), ((), ())), precision=top_precision, preferred_element_type=jnp.float32)
         couple_ref[...] = jnp.dot(half, hot, precision=top_precision, preferred_element_type=jnp.float32)
 
+    loads[2].wait()
     build_source(me)
+    for load in loads[3:]:
+        load.wait()
     build_coupling()
-    for load in loads:
-        load.wait()
     build_potential()
-
-    def build_step(mask, carry):
+    for mask in range(1, group):
         spread_copy(mask, *keys, True).wait()
         build_source(peer_of(mask))
-        return carry
-
-    lax.fori_loop(1, group, build_step, 0)
 
     def stack_rows(pieces):
         return jnp.concatenate(pieces, axis=0)
 
-    cells = stack_rows([krecv[s] for s in range(group)])
+    cells = stack_rows([cell_row(s) for s in range(group)])
     owner = lax.broadcasted_iota(jnp.int32, (group, pw), 0).astype(jnp.float32)
     kin_ref[...] = kinetic(*numbers(cells), owner)
     spread_wait(*firsts)
     for part in range(2):
-        in_vec[0, part] = stack_rows([xrecv[s, part:part + 1] for s in range(group)])
+        in_vec[0, part] = stack_rows([xrecv[s, part] for s in range(group)])
 
     upper = lax.broadcasted_iota(jnp.int32, (8, 128), 0) < 4
     flip = jnp.where(upper, 1.0, -1.0).astype(jnp.float32)
@@ -668,21 +669,35 @@
             send_sem=rs_sem.at[turn, mask - 1], recv_sem=rr_sem.at[turn, mask - 1],
             device_id={"ga": peer_of(mask)}, device_id_type=MESH)
 
-    def take(turn, mask):
+    def take_tile(mask, at):
+        return bdot(left_ref[peer_of(mask)], hot_ref[peer_of(mask), :, at:at + WIDE])
+
+    def take_sum(turn, mask, at, out):
         dest = peer_of(mask)
-        stacked = left_ref[dest]
-        for at in range(0, pw, WIDE):
-            span = slice(at, at + WIDE)
-            out = bdot(stacked, hot_ref[dest, :, span])
-            fold = group_ref[dest, :, span]
-            chosen = out[:2 * slab]
-            for k in range(1, folds):
-                chosen = jnp.where(fold == float(k), out[k * 2 * slab:(k + 1) * 2 * slab], chosen)
-            value = chosen[:slab] + chosen[slab:]
-            for part, table in enumerate((ta_ref, tb_ref)):
-                rsend[turn, mask, part:part + 1, span] = jnp.sum(table[dest, :, span] * value, axis=0, keepdims=True)
-        if mask:
-            partial_copy(turn, mask).start()
+        span = slice(at, at + WIDE)
+        fold = group_ref[dest, :, span]
+        chosen = out[:2 * slab]
+        for k in range(1, folds):
+            chosen = jnp.where(fold == float(k), out[k * 2 * slab:(k + 1) * 2 * slab], chosen)
+        value = chosen[:slab] + chosen[slab:]
+        for part, table in enumerate((ta_ref, tb_ref)):
+            rsend[turn, mask, part:part + 1, span] = jnp.sum(table[dest, :, span] * value, axis=0, keepdims=True)
+
+    def take_all(turn):
+        order = ((6, 7), (2, 3), (4, 5), (1, 0))
+        units = [(masks, mask, at) for masks in order for mask in masks for at in range(0, pw, WIDE)]
+        lag = 3
+        pending = []
+        for unit in units + [None] * lag:
+            if unit:
+                pending.append((unit, take_tile(*unit[1:])))
+            if len(pending) > lag or not unit:
+                (masks, mask, at), out = pending.pop(0)
+                take_sum(turn, mask, at, out)
+                if mask == masks[-1] and at + WIDE == pw:
+                    for ready in masks:
+                        if ready:
+                            partial_copy(turn, ready).start()
 
     def sum_copy(off, send, recv, send_sem, recv_sem, incoming):
         source = lax.rem(me + group - off, group) if incoming else me
@@ -735,11 +750,9 @@
             forward_pair(turn, s)
         for v in range(planes):
             middle(v)
-        for masks in ((6, 7, 2, 3), (4, 5, 1, 0)):
-            for mask in masks[:2]:
-                backward_pair(lax.rem(peer_of(mask), half))
-            for mask in masks:
-                take(turn, mask)
+        for s in range(half):
+            backward_pair(s)
+        take_all(turn)
         start = nonlocal_rows(all_sum_end(*sums) * (1.0 / total_pw))
         own_kin = kin_ref[pl.ds(me, 1), :]
         start = start + own_kin * jnp.concatenate([own_row(in_vec, turn, 0), own_row(in_vec, turn, 1)], axis=0)
@@ -919,6 +932,8 @@
     resid = combine([(1.0, ham_new), (-energy, new_map)])
     resid_norm = gram_form(gram, resid, resid, False) / norm_new
     new_ref[...] = nsend[0] + lam_one * nsend[1]
+    stores = [pltpu.make_async_copy(new_ref, new_hbm, in_sem.at[0]), pltpu.make_async_copy(scal_ref, scal_hbm, in_sem.at[1])]
+    stores[0].start()
     share_end(2, lsend, lrecv)
     summed = all_sum_end(*crossed) * (1.0 / total_pw)
     lam_rows = stack_rows([lrecv[o] for o in range(bands)])
@@ -927,6 +942,9 @@
     scal_ref[...] = jnp.concatenate([
         result, jnp.broadcast_to(energy, (1, 128)), jnp.broadcast_to(resid_norm, (1, 128)),
         jnp.zeros((scal_ref.shape[0] - bands - 2, 128), jnp.float32)], axis=0)
+    stores[1].start()
+    for store in stores:
+        store.wait()
 
 
 def finish_kernel(bands, new_ref, scal_ref, bands_ref, energy_ref, norm_ref, corr_ref, sub_ref):
@@ -967,8 +985,8 @@
             jax.ShapeDtypeStruct((2, pw), f32),
             jax.ShapeDtypeStruct((scal_rows, 128), f32),
         ),
-        in_specs=[vmem, vmem, far, far] + [vmem] * 5,
-        out_specs=(vmem, vmem),
+        in_specs=[far] * 9,
+        out_specs=(far, far),
         scratch_shapes=[
             pltpu.VMEM((group, WIDE, pw), b16),
             pltpu.VMEM((group, folds, 16, pw), b16),
@@ -985,9 +1003,13 @@
             pltpu.VMEM((3, 2, group, pw), f32),
             pltpu.VMEM((2, 2, group, pw), f32),
             pltpu.VMEM((24, 128), f32),
-            dma((2,)),
-            pltpu.VMEM((1, pw), f32), pltpu.VMEM((group, 1, pw), f32),
-            pltpu.VMEM((2, pw), f32), pltpu.VMEM((group, 2, pw), f32),
+            pltpu.VMEM((strengths.shape[0] * strengths.shape[1], strengths.shape[2]), f32),
+            pltpu.VMEM((1, proj_atom.shape[0]), jnp.int32), pltpu.VMEM((1, proj_chan.shape[0]), jnp.int32),
+            pltpu.VMEM(tables[0].shape[1:], b16), pltpu.VMEM(tables[1].shape, b16),
+            pltpu.VMEM((2, pw), f32), pltpu.VMEM((scal_rows, 128), f32),
+            dma((9,)),
+            pltpu.VMEM((pw // 128, 128), jnp.int32), pltpu.VMEM((group, pw // 128, 128), jnp.int32),
+            pltpu.VMEM((2, 1, pw), f32), pltpu.VMEM((group, 2, 1, pw), f32),
             pltpu.VMEM((3, group, 2, pw), f32), pltpu.VMEM((3, group, 2, pw), f32),
             pltpu.VMEM((3, 2, pw), f32), pltpu.VMEM((2, group, 2, pw), f32),
             pltpu.VMEM((3, 2, proj_rows), f32), pltpu.VMEM((3, group, 2, proj_rows), f32),

time: 67.9 us -> 65.2 us (0.960)
  Pallas kernels: 67.1 us -> 64.2 us
    pallas_call x1, Pallas kernels: 65.7 us -> 62.8 us  [kernel_body(): pl.pallas_call(functools.partial(sweep_kernel, (group, bands, planes, gri...]
where the time goes in v3:
time: 65.2 us; the launch traced here: 65 us
  Pallas kernels  64.2 us (98%)
  between operations  0.8 us (1%)
    pallas_call x1, Pallas kernels, kernel_body(): pl.pallas_call(functools.partial(sweep_kernel, (group, bands, planes, gri...  62.8 us
    pallas_call x1, Pallas kernels, kernel_body(): pl.pallas_call(functools.partial(finish_kernel, bands), out_shape=(jax.Sh...  1.39 us

profile of v3, /device:TPU:0, one launch (start us, length us, event | category | flops | bytes accessed | tf_op | source)
XLA Modules:
  0.0 65.0 jit_solution(17965410157949836999)
XLA Ops:
  0.6 62.8 %sweeps.1 = (f32[2,2304]{1,0:T(2,128)}, f32[8,128]{1,0:T(8,128)}) custom-call(f32[2,1,2304]{2,1,0:T(1,128)} %coeffs_hbm.1, s32[18,128]{1,0:T(8,128)} %bitcast.11, f32[1152,96]{1,0:T(8,128)} %bitcast.9, f32[128,2304]{1,0:T(8,128)} %bitcast.8, f32[64,8]{1,0:T(8,128)} %bitcast.10, s32[1,64]{1,0:T(1,128)} %bitcast.12, s32[1,64]{1,0:T(1,128)} %bitcast.13, ...), custom_call_target="tpu_custom_call" | custom-call | tf_op jit(solution)/shard_map/sweeps/pallas_call | solution.py:982
  63.4 1.4 %finish.1 = (f32[2,1,2304]{2,1,0:T(1,128)}, f32[1]{0:T(128)}, f32[1]{0:T(128)}, f32[2,1,4]{2,1,0:T(1,128)}, f32[2,1,4]{2,1,0:T(1,128)}) custom-call(f32[2,2304]{1,0:T(2,128)} %get-tuple-element.7.new_ref, f32[8,128]{1,0:T(8,128)} %get-tuple-element.8.scal_ref), custom_call_target="tpu_custom_call" | custom-call | tf_op jit(solution)/shard_map/finish/pallas_call | solution.py:1037

commit v4 on v3

--- a/solution.py
+++ b/solution.py
@@ -310,17 +310,12 @@
 def const_tables(grid_len, group):
     planes = grid_len // group
     unit = 2.0 * np.pi / grid_len
-    quarter = grid_len / 4.0
-    main = list(range(8))
-    rest = list(range(8, planes))
-    y_in = np.array(main + rest + rest + main)
-    part_row = np.array([0] * planes + [1] * planes)
-    y_real = np.arange(group)[:, None] * planes + y_in[None, :]
     freq = np.arange(grid_len)
-    phase = (y_real[..., None] * freq) % grid_len
-    tab_a = np.cos(unit * (phase - quarter * part_row[:, None]))
-    tab_b = np.cos(unit * (phase + quarter * (1 - part_row[:, None])))
-    high, low = split_const(np.concatenate([tab_a, tab_b], axis=1))
+    y_real = np.arange(group)[:, None] * planes + np.arange(planes)[None, :]
+    phase = unit * ((y_real[..., None] * freq) % grid_len)
+    cos_y, sin_y = np.cos(phase), np.sin(phase)
+    high, low = split_const(np.concatenate([
+        cos_y[:, :8], sin_y[:, :8], cos_y[:, 8:], sin_y[:, 8:], -sin_y[:, 8:], cos_y[:, 8:]], axis=1))
     wave = np.concatenate([high, low], axis=2)
     theta = unit * (np.outer(freq, freq) % grid_len)
     turn = np.zeros((2, 128, 2, 128))
@@ -413,7 +408,7 @@
     coeffs_hbm, cell_hbm, potential_hbm, proj_hbm, strength_hbm, atom_hbm, chan_hbm,
     wave_hbm, zed_hbm,
     new_hbm, scal_hbm,
-    hot_ref, mask_ref, group_ref, ta_ref, tb_ref, kin_ref, work_ref, left_ref,
+    hot_ref, fold_ref, group_ref, phase_ref, kin_ref, work_ref, left_ref,
     pot_ref, potential_ref, proj_ref, couple_ref, in_vec, out_vec, save_ref,
     strength_ref, atom_ref, chan_ref, wave_ref, zed_ref, new_ref, scal_ref, in_sem,
     ksend, krecv, xsend, xrecv, rsend, rrecv, hsend, hrecv, psend, precv,
@@ -423,8 +418,10 @@
 ):
     group, bands, planes, grid_len, total_pw, pw = dims
     slab = 2 * planes
-    folds = planes // 2
+    folds = planes // 2 - 1
     half = group // 2
+    gap = 128 - grid_len
+    splits = grid_len // gap
     tiles = pw // 128
     me = lax.axis_index("ga")
     band = lax.axis_index("band")
@@ -451,6 +448,7 @@
         load.wait()
 
     far_first = (6, 7, 4, 5, 2, 3, 1)
+    near_first = (2, 4, 3, 5, 6, 7, 1)
 
     def spread_copy(mask, send, recv, send_sem, recv_sem, incoming):
         peer = peer_of(mask)
@@ -459,8 +457,8 @@
             send_sem=send_sem.at[mask - 1], recv_sem=recv_sem.at[mask - 1],
             device_id={"ga": peer}, device_id_type=MESH)
 
-    def spread_start(send, recv, send_sem, recv_sem):
-        for mask in far_first:
+    def spread_start(order, send, recv, send_sem, recv_sem):
+        for mask in order:
             spread_copy(mask, send, recv, send_sem, recv_sem, False).start()
 
     def spread_wait(send, recv, send_sem, recv_sem):
@@ -470,8 +468,8 @@
     keys = (ksend, krecv, ks_sem, kr_sem)
     firsts = (xsend, xrecv, xs_sem, xr_sem)
     pl.semaphore_wait(barrier, group + bands - 2)
-    spread_start(*keys)
-    spread_start(*firsts)
+    spread_start(near_first, *keys)
+    spread_start(near_first, *firsts)
     krecv[me] = ksend[...]
     xrecv[me] = xsend[...]
 
@@ -504,18 +502,21 @@
 
     def build_source(src):
         plane, y_num, z_num = numbers(cell_row(src))
-        fold = whole((plane + 0.5) * 0.5)
+        pair = whole((plane + 0.5) * 0.5)
+        piece = whole((z_num + 0.5) * (1.0 / gap))
+        hole = (plane - 2.0 * folds) * splits + piece
+        hole_pair = whole((hole + 0.5) * 0.5)
+        main = plane < 2.0 * folds
+        fold = jnp.where(main, pair, hole_pair)
+        lane = jnp.where(
+            main, (plane - 2.0 * pair) * 128.0 + z_num,
+            (hole - 2.0 * hole_pair) * 128.0 + grid_len + z_num - gap * piece)
         group_ref[src] = fold
-        for k, piece in enumerate(marks((plane - 2.0 * fold) * 128.0 + z_num, WIDE // 16)):
-            hot_ref[src, 16 * k:16 * (k + 1), :] = piece
-        wide_fold = jnp.broadcast_to(fold, (16, pw)).astype(jnp.bfloat16)
-        one, zero = jnp.ones((16, pw), jnp.bfloat16), jnp.zeros((16, pw), jnp.bfloat16)
-        for k in range(folds):
-            mask_ref[src, k] = jnp.where(wide_fold == float(k), one, zero)
+        fold_ref[src] = jnp.broadcast_to(fold, (16, pw)).astype(jnp.bfloat16)
+        for k, rows in enumerate(marks(lane, WIDE // 16)):
+            hot_ref[src, 16 * k:16 * (k + 1), :] = rows
         y_hot = marks(y_num, grid_len // 16)
-        table = bdot(wave_ref[...], jnp.concatenate(y_hot + y_hot, axis=0))
-        ta_ref[src] = table[:slab]
-        tb_ref[src] = table[slab:]
+        phase_ref[src] = bdot(wave_ref[...], jnp.concatenate(y_hot + y_hot, axis=0))
 
     def build_potential():
         pad = jnp.zeros((8, 128 - grid_len), jnp.float32)
@@ -549,10 +550,13 @@
 
     loads[2].wait()
     build_source(me)
-    for load in loads[3:]:
+    for load in loads[3:6]:
         load.wait()
     build_coupling()
+    loads[6].wait()
     build_potential()
+    loads[7].wait()
+    loads[8].wait()
     for mask in range(1, group):
         spread_copy(mask, *keys, True).wait()
         build_source(peer_of(mask))
@@ -568,6 +572,7 @@
         in_vec[0, part] = stack_rows([xrecv[s, part] for s in range(group)])
 
     upper = lax.broadcasted_iota(jnp.int32, (8, 128), 0) < 4
+    lane_at = lax.broadcasted_iota(jnp.int32, (8, 128), 1)
     flip = jnp.where(upper, 1.0, -1.0).astype(jnp.float32)
 
     def swap_half(values):
@@ -607,11 +612,16 @@
 
     def put(turn, src):
         v_re, v_im = in_vec[turn, 0, src:src + 1, :], in_vec[turn, 1, src:src + 1, :]
-        both = split_rows(ta_ref[src] * v_re + tb_ref[src] * v_im)
+        cos_y, sin_y, mix_re, mix_im = [phase_ref[src, 8 * k:8 * k + 8, :] for k in range(4)]
+        both = split_rows(jnp.concatenate([
+            cos_y * v_re - sin_y * v_im, mix_re * v_re + mix_im * v_im, sin_y * v_re + cos_y * v_im], axis=0))
         pieces = []
+        fold = fold_ref[src]
+        blank = jnp.zeros((16, pw), jnp.bfloat16)
         for k in range(folds):
+            hit = fold == float(k)
             for at in range(0, 2 * slab, 16):
-                pieces.append(both[at:at + 16] * mask_ref[src, k])
+                pieces.append(jnp.where(hit, both[at:at + 16], blank))
         out = bdot_t(jnp.concatenate(pieces, axis=0), hot_ref[src])
         tiles = []
         for k in range(folds):
@@ -619,6 +629,15 @@
             block = out[base:base + slab] + out[base + slab:base + 2 * slab]
             for at in (0, 128):
                 tiles.append([block[8 * t:8 * t + 8, at:at + 128] for t in range(3)])
+        for extra in range(planes - 2 * folds):
+            joined = []
+            for t in range(3):
+                run = None
+                for q in reversed(range(splits)):
+                    moved = pltpu.roll(tiles[extra * splits + q][t], (q + 1) * gap, 1)
+                    run = moved if run is None else jnp.where(lane_at < (q + 1) * gap, moved, run)
+                joined.append(run)
+            tiles.append(joined)
         return tiles
 
     def forward_pair(turn, s):
@@ -659,6 +678,11 @@
         low = [(a[0], jnp.where(upper, r[0], swap_half(r[1])), a[1]) for a, r in zip(low, rest)]
         high = [(b[0], jnp.where(upper, swap_half(r[0]), r[1]), b[1]) for b, r in zip(high, rest)]
         for dest, tiles in ((s, low), (s + half, high)):
+            for hole in range((planes - 2 * folds) * splits):
+                extra, q = 2 * folds + hole // splits, hole % splits
+                tiles[hole] = tuple(
+                    jnp.where(lane_at >= grid_len, pltpu.roll(tiles[extra][t], grid_len - q * gap, 1), tiles[hole][t])
+                    for t in range(3))
             for k in range(folds):
                 block = jnp.concatenate([jnp.concatenate(tiles[2 * k + m], axis=0) for m in range(2)], axis=1)
                 left_ref[dest, k * 2 * slab:(k + 1) * 2 * slab, :] = split_rows(block)
@@ -680,8 +704,12 @@
         for k in range(1, folds):
             chosen = jnp.where(fold == float(k), out[k * 2 * slab:(k + 1) * 2 * slab], chosen)
         value = chosen[:slab] + chosen[slab:]
-        for part, table in enumerate((ta_ref, tb_ref)):
-            rsend[turn, mask, part:part + 1, span] = jnp.sum(table[dest, :, span] * value, axis=0, keepdims=True)
+        first, mixed, last = [value[8 * k:8 * k + 8] for k in range(3)]
+        cos_y, sin_y, mix_re, mix_im = [phase_ref[dest, 8 * k:8 * k + 8, span] for k in range(4)]
+        back_re = cos_y * first + sin_y * last + mix_re * mixed
+        back_im = cos_y * last - sin_y * first + mix_im * mixed
+        for part, back in enumerate((back_re, back_im)):
+            rsend[turn, mask, part:part + 1, span] = jnp.sum(back, axis=0, keepdims=True)
 
     def take_all(turn):
         order = ((6, 7), (2, 3), (4, 5), (1, 0))
@@ -745,13 +773,13 @@
 
     def apply_h(turn):
         sums = (psend.at[turn], precv.at[turn], ps_sem.at[turn], pr_sem.at[turn])
-        all_sum(project(turn), *sums)
         for s in range(half):
             forward_pair(turn, s)
         for v in range(planes):
             middle(v)
         for s in range(half):
             backward_pair(s)
+        all_sum(project(turn), *sums)
         take_all(turn)
         start = nonlocal_rows(all_sum_end(*sums) * (1.0 / total_pw))
         own_kin = kin_ref[pl.ds(me, 1), :]
@@ -765,7 +793,7 @@
 
     def share_h(turn):
         out = (hsend.at[turn], hrecv.at[turn], hs_sem.at[turn], hr_sem.at[turn])
-        spread_start(*out)
+        spread_start(far_first, *out)
         hrecv[turn, me] = hsend[turn]
         spread_wait(*out)
         for part in range(2):
@@ -969,7 +997,7 @@
     pw = coeffs.shape[2]
     total_pw = pw * group
     slab = 2 * planes
-    folds = planes // 2
+    folds = planes // 2 - 1
     tile_count = group + group // 2
     proj_rows = 2 * projectors.shape[1]
     tables = [jnp.asarray(t) for t in const_tables(grid_len, group)]
@@ -989,10 +1017,9 @@
         out_specs=(far, far),
         scratch_shapes=[
             pltpu.VMEM((group, WIDE, pw), b16),
-            pltpu.VMEM((group, folds, 16, pw), b16),
+            pltpu.VMEM((group, 16, pw), b16),
             pltpu.VMEM((group, 1, pw), f32),
-            pltpu.VMEM((group, slab, pw), f32),
-            pltpu.VMEM((group, slab, pw), f32),
+            pltpu.VMEM((group, 32, pw), f32),
             pltpu.VMEM((group, pw), f32),
             pltpu.VMEM((2, planes, tile_count, 8, 128), f32),
             pltpu.VMEM((group, folds * 2 * slab, WIDE), b16),

time: 65.2 us -> 63.7 us (0.977)
  Pallas kernels: 64.2 us -> 62.7 us
    pallas_call x1, Pallas kernels: 62.8 us -> 61.3 us  [kernel_body(): pl.pallas_call(functools.partial(sweep_kernel, (group, bands, planes, gri...]
where the time goes in v4:
time: 63.7 us; the launch traced here: 63.5 us
  Pallas kernels  62.7 us (98%)
  between operations  0.8 us (1%)
    pallas_call x1, Pallas kernels, kernel_body(): pl.pallas_call(functools.partial(sweep_kernel, (group, bands, planes, gri...  61.3 us
    pallas_call x1, Pallas kernels, kernel_body(): pl.pallas_call(functools.partial(finish_kernel, bands), out_shape=(jax.Sh...  1.39 us

profile of v4, /device:TPU:0, one launch (start us, length us, event | category | flops | bytes accessed | tf_op | source)
XLA Modules:
  0.0 63.5 jit_solution(14983787556283732775)
XLA Ops:
  0.6 61.3 %sweeps.1 = (f32[2,2304]{1,0:T(2,128)}, f32[8,128]{1,0:T(8,128)}) custom-call(f32[2,1,2304]{2,1,0:T(1,128)} %coeffs_hbm.1, s32[18,128]{1,0:T(8,128)} %bitcast.11, f32[1152,96]{1,0:T(8,128)} %bitcast.9, f32[128,2304]{1,0:T(8,128)} %bitcast.8, f32[64,8]{1,0:T(8,128)} %bitcast.10, s32[1,64]{1,0:T(1,128)} %bitcast.12, s32[1,64]{1,0:T(1,128)} %bitcast.13, ...), custom_call_target="tpu_custom_call" | custom-call | tf_op jit(solution)/shard_map/sweeps/pallas_call | solution.py:1010
  62.0 1.4 %finish.1 = (f32[2,1,2304]{2,1,0:T(1,128)}, f32[1]{0:T(128)}, f32[1]{0:T(128)}, f32[2,1,4]{2,1,0:T(1,128)}, f32[2,1,4]{2,1,0:T(1,128)}) custom-call(f32[2,2304]{1,0:T(2,128)} %get-tuple-element.7.new_ref, f32[8,128]{1,0:T(8,128)} %get-tuple-element.8.scal_ref), custom_call_target="tpu_custom_call" | custom-call | tf_op jit(solution)/shard_map/finish/pallas_call | solution.py:1064

commit v5 on v4

--- a/solution.py
+++ b/solution.py
@@ -412,9 +412,9 @@
     pot_ref, potential_ref, proj_ref, couple_ref, in_vec, out_vec, save_ref,
     strength_ref, atom_ref, chan_ref, wave_ref, zed_ref, new_ref, scal_ref, in_sem,
     ksend, krecv, xsend, xrecv, rsend, rrecv, hsend, hrecv, psend, precv,
-    gsend, grecv, nsend, nrecv, isend, irecv, lsend, lrecv, csend, crecv,
+    wsend, wrecv, nsend, nrecv, lsend, lrecv, csend, crecv,
     ks_sem, kr_sem, xs_sem, xr_sem, rs_sem, rr_sem, hs_sem, hr_sem, ps_sem, pr_sem,
-    gs_sem, gr_sem, ns_sem, nr_sem, cs_sem, cr_sem,
+    ws_sem, wr_sem, ns_sem, nr_sem, cs_sem, cr_sem,
 ):
     group, bands, planes, grid_len, total_pw, pw = dims
     slab = 2 * planes
@@ -438,10 +438,9 @@
             (zed_hbm, zed_ref)))
     ]
     barrier = pltpu.get_barrier_semaphore()
-    for mask in range(1, group):
-        pl.semaphore_signal(barrier, inc=1, device_id={"ga": peer_of(mask)}, device_id_type=MESH)
-    for off in range(1, bands):
-        pl.semaphore_signal(barrier, inc=1, device_id={"band": lax.rem(band + off, bands)}, device_id_type=MESH)
+    world = [(off, mask) for off in (2, 3, 1, 0) for mask in (7, 6, 5, 4, 3, 2, 1, 0) if off or mask]
+    for off, mask in world:
+        pl.semaphore_signal(barrier, inc=1, device_id={"band": lax.rem(band + off, bands), "ga": peer_of(mask)}, device_id_type=MESH)
     for load in loads:
         load.start()
     for load in loads[:2]:
@@ -467,7 +466,7 @@
 
     keys = (ksend, krecv, ks_sem, kr_sem)
     firsts = (xsend, xrecv, xs_sem, xr_sem)
-    pl.semaphore_wait(barrier, group + bands - 2)
+    pl.semaphore_wait(barrier, group * bands - 1)
     spread_start(near_first, *keys)
     spread_start(near_first, *firsts)
     krecv[me] = ksend[...]
@@ -857,7 +856,10 @@
 
     first_pairs = new_pairs(0, 2, (False, True))
     second_pairs = new_pairs(2, 4, (False, True))
-    gram_pairs = first_pairs + second_pairs
+    third_pairs = new_pairs(4, 5, (False,))
+    last_pairs = new_pairs(5, 6, (False,))
+    gram_pairs = first_pairs + second_pairs + third_pairs
+    lane_id = lax.broadcasted_iota(jnp.int32, (1, 128), 1)
 
     def swap(which, send, recv, off, incoming):
         source = lax.rem(band + bands - off, bands) if incoming else band
@@ -897,7 +899,6 @@
         def _():
             share_h(1)
             gram = gram_sums(second_pairs)
-            save([gram[kind, one, two] for one, two, kind in second_pairs], len(first_pairs))
             for k, (one, two, kind) in enumerate(first_pairs):
                 gram[kind, one, two] = gram[kind, two, one] = load_saved(k)
             psi_mid, h_mid, r_mid, eps_mid, step = second_step(gram)
@@ -905,72 +906,103 @@
             p_one = smooth(realize(r_mid, vector), level)
             in_vec[2] = p_one
             share(0, nsend, nrecv, jnp.stack([realize(psi_mid, own), own(4), realize(h_mid, own)]))
+            gram.update(gram_sums(third_pairs))
+            packed = jnp.zeros((1, 128), jnp.float32)
+            for k, (one, two, kind) in enumerate(gram_pairs):
+                packed = jnp.where(lane_id == k, gram[kind, one, two], packed)
+            share(1, lsend, lrecv, packed)
 
         return carry
 
     lax.fori_loop(0, 3, turn_step, 0)
 
     g_own = hsend[2]
-    share(1, isend, irecv, g_own)
-    last_pairs = new_pairs(4, 6, (False,))
 
     def own_last(index):
         return g_own if index == 5 else own(index)
 
-    lane_id = lax.broadcasted_iota(jnp.int32, (1, 128), 1)
+    def world_copy(off, mask, incoming):
+        source = (lax.rem(band + bands - off, bands) * group + peer_of(mask)) if incoming else band * group + me
+        return pltpu.make_async_remote_copy(
+            src_ref=wsend, dst_ref=wrecv.at[source],
+            send_sem=ws_sem.at[off * group + mask - 1], recv_sem=wr_sem.at[off * group + mask - 1],
+            device_id={"band": lax.rem(band + off, bands), "ga": peer_of(mask)}, device_id_type=MESH)
+
     local = jnp.zeros((1, 128), jnp.float32)
-    held = [own_last(index) for index in range(6)]
     for k, (one, two, kind) in enumerate(last_pairs):
-        local = jnp.where(lane_id == k, total_of(held[one] * held[two]), local)
-    sums = (gsend, grecv, gs_sem, gr_sem)
-    all_sum(local, *sums)
-    gram = {}
-    for k, (one, two, kind) in enumerate(gram_pairs):
-        gram[kind, one, two] = gram[kind, two, one] = load_saved(k)
-    psi_mid, h_mid, r_mid, eps_mid, step = second_step(gram)
-    summed = all_sum_end(*sums) * (1.0 / total_pw)
-    for k, (one, two, kind) in enumerate(last_pairs):
-        gram[kind, one, two] = gram[kind, two, one] = summed[:, k:k + 1]
-    q_one = combine([(1.0, {5: 1.0}), (-eps_mid, {4: 1.0})])
-    lam_one = -gram_form(gram, r_mid, q_one, False) / (gram_form(gram, q_one, q_one, False) + small_eps)
-    share(2, lsend, lrecv, jnp.broadcast_to(lam_one, (1, 128)))
+        local = jnp.where(lane_id == k, total_of(own_last(one) * g_own), local)
+    wsend[...] = local
+    for off, mask in world:
+        world_copy(off, mask, False).start()
+    wrecv[band * group + me] = local
+
     share_end(0, nsend, nrecv)
-    share_end(1, isend, irecv)
-
-    pairs = [
-        [stack_rows([nrecv[o, 0, part:part + 1] for o in range(bands)] + [nrecv[o, 1, part:part + 1] for o in range(bands)]) for part in range(2)],
-        [stack_rows([nrecv[o, 2, part:part + 1] for o in range(bands)] + [irecv[o, part:part + 1] for o in range(bands)]) for part in range(2)],
-    ]
+    others = [[stack_rows([nrecv[o, which, part:part + 1] for o in range(bands)]) for part in range(2)] for which in range(3)]
+    mine = [[nsend[which, part:part + 1] for part in range(2)] for which in range(3)] + [[g_own[0:1], g_own[1:2]]]
+
+    def joined(first, second):
+        return [jnp.concatenate([first[part], second[part]], axis=0) for part in range(2)]
+
+    def twice(first, second):
+        return [jnp.concatenate([jnp.broadcast_to(first[part], (bands, pw)), jnp.broadcast_to(second[part], (bands, pw))], axis=0) for part in range(2)]
+
     column_id = lax.broadcasted_iota(jnp.int32, (2 * bands, 128), 1)
     local = jnp.zeros((2 * bands, 128), jnp.float32)
     slot = 0
-    for o_re, o_im in pairs:
-        for mine in (0, 1):
-            m_re, m_im = nsend[mine, 0:1], nsend[mine, 1:2]
-            for product in (m_re * o_re + m_im * o_im, m_re * o_im - m_im * o_re):
+    for o_row, m_rows in (
+        (joined(others[0], others[1]), (twice(mine[0], mine[0]), twice(mine[1], mine[1]))),
+        (joined(others[2], others[1]), (twice(mine[0], mine[2]), twice(mine[1], mine[3]))),
+    ):
+        for m_re, m_im in m_rows:
+            for product in (m_re * o_row[0] + m_im * o_row[1], m_re * o_row[1] - m_im * o_row[0]):
                 local = jnp.where(column_id == slot, jnp.sum(product, axis=1, keepdims=True), local)
                 slot += 1
     crossed = (csend, crecv, cs_sem, cr_sem)
     all_sum(local, *crossed)
 
+    share_end(1, lsend, lrecv)
+    early = stack_rows([lrecv[o] for o in range(bands)])
+    gram = {}
+    for k, (one, two, kind) in enumerate(gram_pairs):
+        gram[kind, one, two] = gram[kind, two, one] = early[:, k:k + 1]
+    psi_mid, h_mid, r_mid, eps_mid, step = second_step(gram)
+    for off, mask in world:
+        world_copy(off, mask, True).wait_recv()
+    late = []
+    for other in range(bands):
+        running = wrecv[other * group]
+        for dev in range(1, group):
+            running = running + wrecv[other * group + dev]
+        late.append(running)
+    late = stack_rows(late) * (1.0 / total_pw)
+    for k, (one, two, kind) in enumerate(last_pairs):
+        gram[kind, one, two] = gram[kind, two, one] = late[:, k:k + 1]
+    q_one = combine([(1.0, {5: 1.0}), (-eps_mid, {4: 1.0})])
+    lam_one = -gram_form(gram, r_mid, q_one, False) / (gram_form(gram, q_one, q_one, False) + small_eps)
+    own_band = lax.broadcasted_iota(jnp.int32, (bands, 1), 0) == band
+
+    def pick(column):
+        return jnp.sum(jnp.where(own_band, column, 0.0), axis=0, keepdims=True)
+
+    own_lam = pick(lam_one)
+    new_ref[...] = nsend[0] + own_lam * nsend[1]
+    stores = [pltpu.make_async_copy(new_ref, new_hbm, in_sem.at[0]), pltpu.make_async_copy(scal_ref, scal_hbm, in_sem.at[1])]
+    stores[0].start()
     new_map = combine([(1.0, psi_mid), (lam_one, {4: 1.0})])
     ham_new = combine([(1.0, h_mid), (lam_one, {5: 1.0})])
     norm_new = gram_form(gram, new_map, new_map, False) + small_eps
     energy = gram_form(gram, new_map, ham_new, False) / norm_new
     resid = combine([(1.0, ham_new), (-energy, new_map)])
     resid_norm = gram_form(gram, resid, resid, False) / norm_new
-    new_ref[...] = nsend[0] + lam_one * nsend[1]
-    stores = [pltpu.make_async_copy(new_ref, new_hbm, in_sem.at[0]), pltpu.make_async_copy(scal_ref, scal_hbm, in_sem.at[1])]
-    stores[0].start()
-    share_end(2, lsend, lrecv)
     summed = all_sum_end(*crossed) * (1.0 / total_pw)
-    lam_rows = stack_rows([lrecv[o] for o in range(bands)])
-    mixed = summed[:bands] + lam_rows * summed[bands:]
-    result = mixed + lam_one * pltpu.roll(mixed, 126, 1)
+    mixed = summed[:bands] + lam_one * summed[bands:]
+    result = mixed + own_lam * pltpu.roll(mixed, 126, 1)
     scal_ref[...] = jnp.concatenate([
-        result, jnp.broadcast_to(energy, (1, 128)), jnp.broadcast_to(resid_norm, (1, 128)),
+        result, jnp.broadcast_to(pick(energy), (1, 128)), jnp.broadcast_to(pick(resid_norm), (1, 128)),
         jnp.zeros((scal_ref.shape[0] - bands - 2, 128), jnp.float32)], axis=0)
     stores[1].start()
+    for off, mask in world:
+        world_copy(off, mask, True).wait_send()
     for store in stores:
         store.wait()
 
@@ -1040,15 +1072,14 @@
             pltpu.VMEM((3, group, 2, pw), f32), pltpu.VMEM((3, group, 2, pw), f32),
             pltpu.VMEM((3, 2, pw), f32), pltpu.VMEM((2, group, 2, pw), f32),
             pltpu.VMEM((3, 2, proj_rows), f32), pltpu.VMEM((3, group, 2, proj_rows), f32),
-            pltpu.VMEM((1, 128), f32), pltpu.VMEM((group, 1, 128), f32),
+            pltpu.VMEM((1, 128), f32), pltpu.VMEM((bands * group, 1, 128), f32),
             pltpu.VMEM((3, 2, pw), f32), pltpu.VMEM((bands, 3, 2, pw), f32),
-            pltpu.VMEM((2, pw), f32), pltpu.VMEM((bands, 2, pw), f32),
             pltpu.VMEM((1, 128), f32), pltpu.VMEM((bands, 1, 128), f32),
             pltpu.VMEM((2 * bands, 128), f32), pltpu.VMEM((group, 2 * bands, 128), f32),
             dma((peers,)), dma((peers,)), dma((peers,)), dma((peers,)),
             dma((3, peers)), dma((3, peers)), dma((2, peers)), dma((2, peers)),
-            dma((3, peers)), dma((3, peers)), dma((peers,)), dma((peers,)),
-            dma((3, bands - 1)), dma((3, bands - 1)), dma((peers,)), dma((peers,)),
+            dma((3, peers)), dma((3, peers)), dma((bands * group - 1,)), dma((bands * group - 1,)),
+            dma((2, bands - 1)), dma((2, bands - 1)), dma((peers,)), dma((peers,)),
         ],
         compiler_params=pltpu.CompilerParams(
             collective_id=0, has_side_effects=True, vmem_limit_bytes=60 * 1024 * 1024

time: 63.7 us -> 62.1 us (0.975)
  Pallas kernels: 62.7 us -> 61.1 us
    pallas_call x1, Pallas kernels: 61.3 us -> 59.7 us  [kernel_body(): pl.pallas_call(functools.partial(sweep_kernel, (group, bands, planes, gri...]
where the time goes in v5:
time: 62.1 us; the launch traced here: 61.9 us
  Pallas kernels  61.1 us (98%)
  between operations  0.8 us (1%)
    pallas_call x1, Pallas kernels, kernel_body(): pl.pallas_call(functools.partial(sweep_kernel, (group, bands, planes, gri...  59.7 us
    pallas_call x1, Pallas kernels, kernel_body(): pl.pallas_call(functools.partial(finish_kernel, bands), out_shape=(jax.Sh...  1.39 us

profile of v5, /device:TPU:0, one launch (start us, length us, event | category | flops | bytes accessed | tf_op | source)
XLA Modules:
  0.0 61.9 jit_solution(11663240503288153903)
XLA Ops:
  0.6 59.7 %sweeps.1 = (f32[2,2304]{1,0:T(2,128)}, f32[8,128]{1,0:T(8,128)}) custom-call(f32[2,1,2304]{2,1,0:T(1,128)} %coeffs_hbm.1, s32[18,128]{1,0:T(8,128)} %bitcast.11, f32[1152,96]{1,0:T(8,128)} %bitcast.9, f32[128,2304]{1,0:T(8,128)} %bitcast.8, f32[64,8]{1,0:T(8,128)} %bitcast.10, s32[1,64]{1,0:T(1,128)} %bitcast.12, s32[1,64]{1,0:T(1,128)} %bitcast.13, ...), custom_call_target="tpu_custom_call" | custom-call | tf_op jit(solution)/shard_map/sweeps/pallas_call | solution.py:1042
  60.4 1.4 %finish.1 = (f32[2,1,2304]{2,1,0:T(1,128)}, f32[1]{0:T(128)}, f32[1]{0:T(128)}, f32[2,1,4]{2,1,0:T(1,128)}, f32[2,1,4]{2,1,0:T(1,128)}) custom-call(f32[2,2304]{1,0:T(2,128)} %get-tuple-element.7.new_ref, f32[8,128]{1,0:T(8,128)} %get-tuple-element.8.scal_ref), custom_call_target="tpu_custom_call" | custom-call | tf_op jit(solution)/shard_map/finish/pallas_call | solution.py:1095

commit v6 on v5

--- a/solution.py
+++ b/solution.py
@@ -449,20 +449,23 @@
     far_first = (6, 7, 4, 5, 2, 3, 1)
     near_first = (2, 4, 3, 5, 6, 7, 1)
 
-    def spread_copy(mask, send, recv, send_sem, recv_sem, incoming):
+    def wait_bytes(ref, sem):
+        pltpu.make_async_copy(ref, ref, sem).wait()
+
+    def spread_copy(mask, send, recv, send_sem, recv_sem):
         peer = peer_of(mask)
         return pltpu.make_async_remote_copy(
-            src_ref=send, dst_ref=recv.at[peer if incoming else me],
-            send_sem=send_sem.at[mask - 1], recv_sem=recv_sem.at[mask - 1],
+            src_ref=send, dst_ref=recv.at[me],
+            send_sem=send_sem.at[0], recv_sem=recv_sem.at[0 if mask > 1 else recv_sem.shape[0] - 1],
             device_id={"ga": peer}, device_id_type=MESH)
 
     def spread_start(order, send, recv, send_sem, recv_sem):
         for mask in order:
-            spread_copy(mask, send, recv, send_sem, recv_sem, False).start()
+            spread_copy(mask, send, recv, send_sem, recv_sem).start()
 
     def spread_wait(send, recv, send_sem, recv_sem):
-        for mask in range(1, group):
-            spread_copy(mask, send, recv, send_sem, recv_sem, True).wait()
+        wait_bytes(recv.at[pl.ds(0, group - 1)], recv_sem.at[0])
+        wait_bytes(recv.at[pl.ds(0, group - 1)], send_sem.at[0])
 
     keys = (ksend, krecv, ks_sem, kr_sem)
     firsts = (xsend, xrecv, xs_sem, xr_sem)
@@ -556,9 +559,12 @@
     build_potential()
     loads[7].wait()
     loads[8].wait()
-    for mask in range(1, group):
-        spread_copy(mask, *keys, True).wait()
+    wait_bytes(krecv.at[pl.ds(0, 1)], kr_sem.at[1])
+    build_source(peer_of(1))
+    wait_bytes(krecv.at[pl.ds(0, group - 2)], kr_sem.at[0])
+    for mask in range(2, group):
         build_source(peer_of(mask))
+    wait_bytes(krecv.at[pl.ds(0, group - 1)], ks_sem.at[0])
 
     def stack_rows(pieces):
         return jnp.concatenate(pieces, axis=0)
@@ -639,8 +645,7 @@
             tiles.append(joined)
         return tiles
 
-    def forward_pair(turn, s):
-        low, high = put(turn, s), put(turn, s + half)
+    def forward_turn(s, low, high):
         rest = [(
             jnp.where(upper, a[1], swap_half(b[1])), jnp.where(upper, swap_half(a[1]), b[1]),
         ) for a, b in zip(low, high)]
@@ -689,7 +694,7 @@
     def partial_copy(turn, mask):
         return pltpu.make_async_remote_copy(
             src_ref=rsend.at[turn, mask], dst_ref=rrecv.at[turn, mask],
-            send_sem=rs_sem.at[turn, mask - 1], recv_sem=rr_sem.at[turn, mask - 1],
+            send_sem=rs_sem.at[0], recv_sem=rr_sem.at[0],
             device_id={"ga": peer_of(mask)}, device_id_type=MESH)
 
     def take_tile(mask, at):
@@ -726,22 +731,13 @@
                         if ready:
                             partial_copy(turn, ready).start()
 
-    def sum_copy(off, send, recv, send_sem, recv_sem, incoming):
-        source = lax.rem(me + group - off, group) if incoming else me
-        return pltpu.make_async_remote_copy(
-            src_ref=send, dst_ref=recv.at[source],
-            send_sem=send_sem.at[off - 1], recv_sem=recv_sem.at[off - 1],
-            device_id={"ga": lax.rem(me + off, group)}, device_id_type=MESH)
-
     def all_sum(local, send, recv, send_sem, recv_sem):
         send[...] = local
         recv[me] = local
-        for off in range(1, group):
-            sum_copy(off, send, recv, send_sem, recv_sem, False).start()
+        spread_start(far_first, send, recv, send_sem, recv_sem)
 
     def all_sum_end(send, recv, send_sem, recv_sem):
-        for off in range(1, group):
-            sum_copy(off, send, recv, send_sem, recv_sem, True).wait()
+        spread_wait(send, recv, send_sem, recv_sem)
         running = recv[0]
         for dev in range(1, group):
             running = running + recv[dev]
@@ -771,9 +767,13 @@
         return jnp.concatenate(found, axis=0)
 
     def apply_h(turn):
-        sums = (psend.at[turn], precv.at[turn], ps_sem.at[turn], pr_sem.at[turn])
+        sums = (psend.at[turn], precv.at[turn], ps_sem, pr_sem)
+        placed = []
         for s in range(half):
-            forward_pair(turn, s)
+            placed.append((s, put(turn, s), put(turn, s + half)))
+            if s:
+                forward_turn(*placed.pop(0))
+        forward_turn(*placed.pop(0))
         for v in range(planes):
             middle(v)
         for s in range(half):
@@ -784,14 +784,15 @@
         own_kin = kin_ref[pl.ds(me, 1), :]
         start = start + own_kin * jnp.concatenate([own_row(in_vec, turn, 0), own_row(in_vec, turn, 1)], axis=0)
         running = start + rsend[turn, 0]
+        wait_bytes(rrecv.at[turn, pl.ds(1, group - 1)], rr_sem.at[0])
+        wait_bytes(rrecv.at[turn, pl.ds(1, group - 1)], rs_sem.at[0])
         for mask in range(1, group):
-            partial_copy(turn, mask).wait()
             running = running + rrecv[turn, mask]
         hsend[turn] = running
         return running
 
     def share_h(turn):
-        out = (hsend.at[turn], hrecv.at[turn], hs_sem.at[turn], hr_sem.at[turn])
+        out = (hsend.at[turn], hrecv.at[turn], hs_sem, hr_sem)
         spread_start(far_first, *out)
         hrecv[turn, me] = hsend[turn]
         spread_wait(*out)
@@ -861,22 +862,21 @@
     gram_pairs = first_pairs + second_pairs + third_pairs
     lane_id = lax.broadcasted_iota(jnp.int32, (1, 128), 1)
 
-    def swap(which, send, recv, off, incoming):
-        source = lax.rem(band + bands - off, bands) if incoming else band
+    def swap(which, send, recv, off):
         return pltpu.make_async_remote_copy(
-            src_ref=send, dst_ref=recv.at[source],
-            send_sem=ns_sem.at[which, off - 1], recv_sem=nr_sem.at[which, off - 1],
+            src_ref=send, dst_ref=recv.at[band],
+            send_sem=ns_sem.at[which], recv_sem=nr_sem.at[which],
             device_id={"band": lax.rem(band + off, bands)}, device_id_type=MESH)
 
     def share(which, send, recv, values):
         send[...] = values
         recv[band] = values
         for off in range(1, bands):
-            swap(which, send, recv, off, False).start()
+            swap(which, send, recv, off).start()
 
     def share_end(which, send, recv):
-        for off in range(1, bands):
-            swap(which, send, recv, off, True).wait()
+        wait_bytes(recv.at[pl.ds(0, bands - 1)], nr_sem.at[which])
+        wait_bytes(recv.at[pl.ds(0, bands - 1)], ns_sem.at[which])
 
     def own(index):
         ref = out_vec if index % 2 else in_vec
@@ -921,11 +921,10 @@
     def own_last(index):
         return g_own if index == 5 else own(index)
 
-    def world_copy(off, mask, incoming):
-        source = (lax.rem(band + bands - off, bands) * group + peer_of(mask)) if incoming else band * group + me
+    def world_copy(off, mask):
         return pltpu.make_async_remote_copy(
-            src_ref=wsend, dst_ref=wrecv.at[source],
-            send_sem=ws_sem.at[off * group + mask - 1], recv_sem=wr_sem.at[off * group + mask - 1],
+            src_ref=wsend, dst_ref=wrecv.at[band * group + me],
+            send_sem=ws_sem.at[0], recv_sem=wr_sem.at[0],
             device_id={"band": lax.rem(band + off, bands), "ga": peer_of(mask)}, device_id_type=MESH)
 
     local = jnp.zeros((1, 128), jnp.float32)
@@ -933,7 +932,7 @@
         local = jnp.where(lane_id == k, total_of(own_last(one) * g_own), local)
     wsend[...] = local
     for off, mask in world:
-        world_copy(off, mask, False).start()
+        world_copy(off, mask).start()
     wrecv[band * group + me] = local
 
     share_end(0, nsend, nrecv)
@@ -966,8 +965,7 @@
     for k, (one, two, kind) in enumerate(gram_pairs):
         gram[kind, one, two] = gram[kind, two, one] = early[:, k:k + 1]
     psi_mid, h_mid, r_mid, eps_mid, step = second_step(gram)
-    for off, mask in world:
-        world_copy(off, mask, True).wait_recv()
+    wait_bytes(wrecv.at[pl.ds(0, group * bands - 1)], wr_sem.at[0])
     late = []
     for other in range(bands):
         running = wrecv[other * group]
@@ -1001,8 +999,7 @@
         result, jnp.broadcast_to(pick(energy), (1, 128)), jnp.broadcast_to(pick(resid_norm), (1, 128)),
         jnp.zeros((scal_ref.shape[0] - bands - 2, 128), jnp.float32)], axis=0)
     stores[1].start()
-    for off, mask in world:
-        world_copy(off, mask, True).wait_send()
+    wait_bytes(wrecv.at[pl.ds(0, group * bands - 1)], ws_sem.at[0])
     for store in stores:
         store.wait()
 
@@ -1038,7 +1035,6 @@
     far = pl.BlockSpec(memory_space=pl.ANY)
     f32, b16 = jnp.float32, jnp.bfloat16
     scal_rows = 8 * (-(-(bands + 2) // 8))
-    peers = group - 1
     new, scal = pl.pallas_call(
         functools.partial(sweep_kernel, (group, bands, planes, grid_len, total_pw, pw)),
         out_shape=(
@@ -1076,10 +1072,8 @@
             pltpu.VMEM((3, 2, pw), f32), pltpu.VMEM((bands, 3, 2, pw), f32),
             pltpu.VMEM((1, 128), f32), pltpu.VMEM((bands, 1, 128), f32),
             pltpu.VMEM((2 * bands, 128), f32), pltpu.VMEM((group, 2 * bands, 128), f32),
-            dma((peers,)), dma((peers,)), dma((peers,)), dma((peers,)),
-            dma((3, peers)), dma((3, peers)), dma((2, peers)), dma((2, peers)),
-            dma((3, peers)), dma((3, peers)), dma((bands * group - 1,)), dma((bands * group - 1,)),
-            dma((2, bands - 1)), dma((2, bands - 1)), dma((peers,)), dma((peers,)),
+            dma((1,)), dma((2,)), dma((1,)), dma((1,)), dma((1,)), dma((1,)), dma((1,)), dma((1,)),
+            dma((1,)), dma((1,)), dma((1,)), dma((1,)), dma((2,)), dma((2,)), dma((1,)), dma((1,)),
         ],
         compiler_params=pltpu.CompilerParams(
             collective_id=0, has_side_effects=True, vmem_limit_bytes=60 * 1024 * 1024

time: 62.1 us -> 58.3 us (0.939)
  Pallas kernels: 61.1 us -> 57.3 us
    pallas_call x1, Pallas kernels: 59.7 us -> 55.9 us  [kernel_body(): pl.pallas_call(functools.partial(sweep_kernel, (group, bands, planes, gri...]
where the time goes in v6:
time: 58.3 us; the launch traced here: 58.1 us
  Pallas kernels  57.3 us (98%)
  between operations  0.8 us (1%)
    pallas_call x1, Pallas kernels, kernel_body(): pl.pallas_call(functools.partial(sweep_kernel, (group, bands, planes, gri...  55.9 us
    pallas_call x1, Pallas kernels, kernel_body(): pl.pallas_call(functools.partial(finish_kernel, bands), out_shape=(jax.Sh...  1.39 us

profile of v6, /device:TPU:0, one launch (start us, length us, event | category | flops | bytes accessed | tf_op | source)
XLA Modules:
  0.0 58.1 jit_solution(4372128126587325740)
XLA Ops:
  0.6 55.9 %sweeps.1 = (f32[2,2304]{1,0:T(2,128)}, f32[8,128]{1,0:T(8,128)}) custom-call(f32[2,1,2304]{2,1,0:T(1,128)} %coeffs_hbm.1, s32[18,128]{1,0:T(8,128)} %bitcast.11, f32[1152,96]{1,0:T(8,128)} %bitcast.9, f32[128,2304]{1,0:T(8,128)} %bitcast.8, f32[64,8]{1,0:T(8,128)} %bitcast.10, s32[1,64]{1,0:T(1,128)} %bitcast.12, s32[1,64]{1,0:T(1,128)} %bitcast.13, ...), custom_call_target="tpu_custom_call" | custom-call | tf_op jit(solution)/shard_map/sweeps/pallas_call | solution.py:1038
  56.5 1.4 %finish.1 = (f32[2,1,2304]{2,1,0:T(1,128)}, f32[1]{0:T(128)}, f32[1]{0:T(128)}, f32[2,1,4]{2,1,0:T(1,128)}, f32[2,1,4]{2,1,0:T(1,128)}) custom-call(f32[2,2304]{1,0:T(2,128)} %get-tuple-element.7.new_ref, f32[8,128]{1,0:T(8,128)} %get-tuple-element.8.scal_ref), custom_call_target="tpu_custom_call" | custom-call | tf_op jit(solution)/shard_map/finish/pallas_call | solution.py:1089

commit v7 on v6

--- a/solution.py
+++ b/solution.py
@@ -449,6 +449,9 @@
     far_first = (6, 7, 4, 5, 2, 3, 1)
     near_first = (2, 4, 3, 5, 6, 7, 1)
 
+    def stage_of(mask):
+        return (mask > 1) + (mask > 5)
+
     def wait_bytes(ref, sem):
         pltpu.make_async_copy(ref, ref, sem).wait()
 
@@ -456,7 +459,7 @@
         peer = peer_of(mask)
         return pltpu.make_async_remote_copy(
             src_ref=send, dst_ref=recv.at[me],
-            send_sem=send_sem.at[0], recv_sem=recv_sem.at[0 if mask > 1 else recv_sem.shape[0] - 1],
+            send_sem=send_sem.at[0], recv_sem=recv_sem.at[0 if recv_sem.shape[0] == 1 else stage_of(mask)],
             device_id={"ga": peer}, device_id_type=MESH)
 
     def spread_start(order, send, recv, send_sem, recv_sem):
@@ -559,11 +562,10 @@
     build_potential()
     loads[7].wait()
     loads[8].wait()
-    wait_bytes(krecv.at[pl.ds(0, 1)], kr_sem.at[1])
-    build_source(peer_of(1))
-    wait_bytes(krecv.at[pl.ds(0, group - 2)], kr_sem.at[0])
-    for mask in range(2, group):
-        build_source(peer_of(mask))
+    for stage, masks in enumerate(((1,), (2, 3, 4, 5), (6, 7))):
+        wait_bytes(krecv.at[pl.ds(0, len(masks))], kr_sem.at[stage])
+        for mask in masks:
+            build_source(peer_of(mask))
     wait_bytes(krecv.at[pl.ds(0, group - 1)], ks_sem.at[0])
 
     def stack_rows(pieces):
@@ -716,9 +718,9 @@
             rsend[turn, mask, part:part + 1, span] = jnp.sum(back, axis=0, keepdims=True)
 
     def take_all(turn):
-        order = ((6, 7), (2, 3), (4, 5), (1, 0))
+        order = ((6, 7), (4, 5), (2, 3), (1, 0))
         units = [(masks, mask, at) for masks in order for mask in masks for at in range(0, pw, WIDE)]
-        lag = 3
+        lag = 6
         pending = []
         for unit in units + [None] * lag:
             if unit:
@@ -1072,7 +1074,7 @@
             pltpu.VMEM((3, 2, pw), f32), pltpu.VMEM((bands, 3, 2, pw), f32),
             pltpu.VMEM((1, 128), f32), pltpu.VMEM((bands, 1, 128), f32),
             pltpu.VMEM((2 * bands, 128), f32), pltpu.VMEM((group, 2 * bands, 128), f32),
-            dma((1,)), dma((2,)), dma((1,)), dma((1,)), dma((1,)), dma((1,)), dma((1,)), dma((1,)),
+            dma((1,)), dma((3,)), dma((1,)), dma((1,)), dma((1,)), dma((1,)), dma((1,)), dma((1,)),
             dma((1,)), dma((1,)), dma((1,)), dma((1,)), dma((2,)), dma((2,)), dma((1,)), dma((1,)),
         ],
         compiler_params=pltpu.CompilerParams(

time: 58.3 us -> 57.1 us (0.979)
  Pallas kernels: 57.3 us -> 56.1 us
    pallas_call x1, Pallas kernels: 55.9 us -> 54.7 us  [kernel_body(): pl.pallas_call(functools.partial(sweep_kernel, (group, bands, planes, gri...]
where the time goes in v7:
time: 57.1 us; the launch traced here: 56.9 us
  Pallas kernels  56.1 us (98%)
  between operations  0.8 us (1%)
    pallas_call x1, Pallas kernels, kernel_body(): pl.pallas_call(functools.partial(sweep_kernel, (group, bands, planes, gri...  54.7 us
    pallas_call x1, Pallas kernels, kernel_body(): pl.pallas_call(functools.partial(finish_kernel, bands), out_shape=(jax.Sh...  1.39 us

profile of v7, /device:TPU:0, one launch (start us, length us, event | category | flops | bytes accessed | tf_op | source)
XLA Modules:
  0.0 56.9 jit_solution(3151675015906484509)
XLA Ops:
  0.6 54.7 %sweeps.1 = (f32[2,2304]{1,0:T(2,128)}, f32[8,128]{1,0:T(8,128)}) custom-call(f32[2,1,2304]{2,1,0:T(1,128)} %coeffs_hbm.1, s32[18,128]{1,0:T(8,128)} %bitcast.11, f32[1152,96]{1,0:T(8,128)} %bitcast.9, f32[128,2304]{1,0:T(8,128)} %bitcast.8, f32[64,8]{1,0:T(8,128)} %bitcast.10, s32[1,64]{1,0:T(1,128)} %bitcast.12, s32[1,64]{1,0:T(1,128)} %bitcast.13, ...), custom_call_target="tpu_custom_call" | custom-call | tf_op jit(solution)/shard_map/sweeps/pallas_call | solution.py:1040
  55.3 1.4 %finish.1 = (f32[2,1,2304]{2,1,0:T(1,128)}, f32[1]{0:T(128)}, f32[1]{0:T(128)}, f32[2,1,4]{2,1,0:T(1,128)}, f32[2,1,4]{2,1,0:T(1,128)}) custom-call(f32[2,2304]{1,0:T(2,128)} %get-tuple-element.7.new_ref, f32[8,128]{1,0:T(8,128)} %get-tuple-element.8.scal_ref), custom_call_target="tpu_custom_call" | custom-call | tf_op jit(solution)/shard_map/finish/pallas_call | solution.py:1091

commit v8 on v7

--- a/solution.py
+++ b/solution.py
@@ -437,11 +437,13 @@
             (atom_hbm, atom_ref), (chan_hbm, chan_ref), (potential_hbm, potential_ref), (proj_hbm, proj_ref),
             (zed_hbm, zed_ref)))
     ]
+    for load in loads[:2]:
+        load.start()
     barrier = pltpu.get_barrier_semaphore()
     world = [(off, mask) for off in (2, 3, 1, 0) for mask in (7, 6, 5, 4, 3, 2, 1, 0) if off or mask]
     for off, mask in world:
         pl.semaphore_signal(barrier, inc=1, device_id={"band": lax.rem(band + off, bands), "ga": peer_of(mask)}, device_id_type=MESH)
-    for load in loads:
+    for load in loads[2:]:
         load.start()
     for load in loads[:2]:
         load.wait()
@@ -786,6 +788,14 @@
         own_kin = kin_ref[pl.ds(me, 1), :]
         start = start + own_kin * jnp.concatenate([own_row(in_vec, turn, 0), own_row(in_vec, turn, 1)], axis=0)
         running = start + rsend[turn, 0]
+        @pl.when(turn == 2)
+        def _():
+            gram = gram_sums(third_pairs)
+            packed = save_ref[8:9, :]
+            for k, (one, two, kind) in enumerate(third_pairs):
+                packed = jnp.where(lane_id == k + len(first_pairs + second_pairs), gram[kind, one, two], packed)
+            share(1, lsend, lrecv, packed)
+
         wait_bytes(rrecv.at[turn, pl.ds(1, group - 1)], rr_sem.at[0])
         wait_bytes(rrecv.at[turn, pl.ds(1, group - 1)], rs_sem.at[0])
         for mask in range(1, group):
@@ -908,11 +918,10 @@
             p_one = smooth(realize(r_mid, vector), level)
             in_vec[2] = p_one
             share(0, nsend, nrecv, jnp.stack([realize(psi_mid, own), own(4), realize(h_mid, own)]))
-            gram.update(gram_sums(third_pairs))
             packed = jnp.zeros((1, 128), jnp.float32)
-            for k, (one, two, kind) in enumerate(gram_pairs):
+            for k, (one, two, kind) in enumerate(first_pairs + second_pairs):
                 packed = jnp.where(lane_id == k, gram[kind, one, two], packed)
-            share(1, lsend, lrecv, packed)
+            save_ref[8:9, :] = packed
 
         return carry
 

time: 57.1 us -> 56.8 us (level)
  no operation moved by 1% of the time
where the time goes in v8:
time: 56.8 us; the launch traced here: 56.6 us
  Pallas kernels  55.8 us (98%)
  between operations  0.8 us (1%)
    pallas_call x1, Pallas kernels, kernel_body(): pl.pallas_call(functools.partial(sweep_kernel, (group, bands, planes, gri...  54.4 us
    pallas_call x1, Pallas kernels, kernel_body(): pl.pallas_call(functools.partial(finish_kernel, bands), out_shape=(jax.Sh...  1.39 us

profile of v8, /device:TPU:0, one launch (start us, length us, event | category | flops | bytes accessed | tf_op | source)
XLA Modules:
  0.0 56.6 jit_solution(6450657006450945121)
XLA Ops:
  0.6 54.4 %sweeps.1 = (f32[2,2304]{1,0:T(2,128)}, f32[8,128]{1,0:T(8,128)}) custom-call(f32[2,1,2304]{2,1,0:T(1,128)} %coeffs_hbm.1, s32[18,128]{1,0:T(8,128)} %bitcast.11, f32[1152,96]{1,0:T(8,128)} %bitcast.9, f32[128,2304]{1,0:T(8,128)} %bitcast.8, f32[64,8]{1,0:T(8,128)} %bitcast.10, s32[1,64]{1,0:T(1,128)} %bitcast.12, s32[1,64]{1,0:T(1,128)} %bitcast.13, ...), custom_call_target="tpu_custom_call" | custom-call | tf_op jit(solution)/shard_map/sweeps/pallas_call | solution.py:1049
  55.0 1.4 %finish.1 = (f32[2,1,2304]{2,1,0:T(1,128)}, f32[1]{0:T(128)}, f32[1]{0:T(128)}, f32[2,1,4]{2,1,0:T(1,128)}, f32[2,1,4]{2,1,0:T(1,128)}) custom-call(f32[2,2304]{1,0:T(2,128)} %get-tuple-element.7.new_ref, f32[8,128]{1,0:T(8,128)} %get-tuple-element.8.scal_ref), custom_call_target="tpu_custom_call" | custom-call | tf_op jit(solution)/shard_map/finish/pallas_call | solution.py:1100
